TPU v7x, 32 devices: a whole 2x2x4 slice. The times are simulated.
32 devices in a mesh: gx: 16 (over z, y, x), gy: 2 (over core).
Axes of the slice: x: 2, y: 2, z: 4, core: 2. Of those that a mesh axis runs over, the one named last changes fastest.
Arguments:
- fields: bfloat16 [4, 1, 3072, 3072], P(None, None, 'gx', 'gy'), may hold values from -6 to 6
- x_codes: int32 [1024], replicated, may hold values from 0 to 1024, as said below
- y_codes: int32 [1020], replicated, may hold values from 0 to 1024, as said below
Outputs:
- spectrum: float32 [4, 1, 1024, 1020], P(None, None, 'gx', 'gy')
- lowpass: float32 [4, 1, 3072, 3072], P(None, None, 'gx', 'gy')
Inputs may be any that keep to these rules, and one draw needn't show every extreme that they name: `x_codes`: distinct codes in rising order, each naming one real Fourier basis function with wavenumber at most 512. `y_codes`: distinct codes in rising order, each naming one real Fourier basis function with wavenumber at most 512.
All inputs are finite; a program needn't handle non-finite values.
Results may differ from a plain program's by a relative error of at most 0.006.
Values may be sent and summed in bfloat16 or wider, within the bound.
A program may use at most 64 MiB of HBM per device.

v0:
```python
import functools
import math

import jax
import jax.numpy as jnp
from jax import lax
from jax.experimental import pallas as pl
from jax.experimental.pallas import tpu as pltpu
from jax.sharding import PartitionSpec as P

NX = 3072
NY = 3072
BAND = 512
STEP = 64


def angle(freq, position, length):
    phase = freq[None, :] * position[:, None] % length
    return phase.astype(jnp.float32) * (2.0 * math.pi / length)


def mode_parts(picked, first, amount, length, live=None):
    step = 64 if amount % 64 == 0 else 8
    freq = jnp.where(picked <= BAND, picked, picked - BAND)
    coarse_angle = angle(freq, first + step * jnp.arange(amount // step, dtype=jnp.int32), length)
    fine_angle = angle(freq, jnp.arange(step, dtype=jnp.int32), length)
    norm = jnp.where(picked == 0, 1.0 / math.sqrt(length), math.sqrt(2.0 / length)).astype(jnp.float32)
    if live is not None:
        norm = jnp.where(live, norm, 0.0)
    is_cos = (picked <= BAND)[None, :]
    c, s = jnp.cos(coarse_angle), jnp.sin(coarse_angle)
    first_part = jnp.where(is_cos, c, s) * norm[None, :]
    second_part = jnp.where(is_cos, -s, c) * norm[None, :]
    fc, fs = jnp.cos(fine_angle), jnp.sin(fine_angle)
    return lax.optimization_barrier((first_part, second_part, fc, fs))


def mode_table(picked, first, amount, length, live=None):
    first_part, second_part, fc, fs = mode_parts(picked, first, amount, length, live)
    table = first_part[:, None, :] * fc[None] + second_part[:, None, :] * fs[None]
    return table.astype(jnp.bfloat16).reshape(amount, picked.shape[0])


def al(v, m):
    return pl.multiple_of(v, m)


def turn(freq, position, shift, length):
    product = freq * position
    quarter = jnp.floor(product * (4.0 / length) + 0.5)
    x = (product * 4.0 - quarter * length) * (2.0 * math.pi / (4 * length))
    x2 = x * x
    s = x + x * x2 * (-1 / 6 + x2 * (1 / 120 + x2 * (-1 / 5040 + x2 * (1 / 362880))))
    c = 1.0 + x2 * (-0.5 + x2 * (1 / 24 + x2 * (-1 / 720 + x2 * (1 / 40320))))
    quarter = quarter - shift
    q = quarter - 4.0 * jnp.floor(quarter * 0.25)
    odd = (q == 1.0) | (q == 3.0)
    cos_value, sin_value = jnp.where(odd, s, c), jnp.where(odd, c, s)
    cos_value = jnp.where((q == 1.0) | (q == 2.0), -cos_value, cos_value)
    return cos_value, jnp.where(q >= 2.0, -sin_value, sin_value)


def make_table(code_ref, first, length, table, ta, tb, fc, fs):
    amount, codes = table.shape
    f32 = jnp.float32
    code = code_ref[...]
    freq = jnp.where(code <= BAND, code, code - BAND).astype(f32)
    shift = jnp.where(code <= BAND, 0, 1).astype(f32)
    norm = jnp.where(code == 0, 1.0 / math.sqrt(length), math.sqrt(2.0 / length)).astype(f32)
    norm = jnp.where(code < 0, 0.0, norm)
    row = lax.broadcasted_iota(jnp.int32, (8, codes), 0)

    @pl.loop(0, amount // STEP // 8)
    def _(i):
        c, s = turn(freq, (first + (row + i * 8) * STEP).astype(f32), shift, length)
        ta[pl.ds(al(i * 8, 8), 8), :] = c * norm
        tb[pl.ds(al(i * 8, 8), 8), :] = s * norm

    @pl.loop(0, STEP // 8)
    def _(i):
        c, s = turn(freq, (row + i * 8).astype(f32), 0.0, length)
        fc[pl.ds(al(i * 8, 8), 8), :] = c
        fs[pl.ds(al(i * 8, 8), 8), :] = s

    @pl.loop(0, amount // STEP)
    def _(h):
        table[pl.ds(al(h * STEP, STEP), STEP), :] = (
            ta[pl.ds(h, 1), :] * fc[...] - tb[pl.ds(h, 1), :] * fs[...]
        ).astype(jnp.bfloat16)


def exchange_kernel(
    gx, lead, x_local, kx, kpad, cols,
    grid_in, xcode_ref, ycode_ref, spec_ref, low_out,
    grid_ref, wide_ref, low_ref, y_ref, ta, tb, fc, fs, other, inc, part, lines, xt, acc, coarse, syn,
    gs, gr, s1, r1, s2, r2, s3, r3, s4, r4, grid_sem, low_sem,
):
    me = lax.axis_index("gx")
    half = lax.axis_index("gy")
    peer = 1 - half
    groups = gx // lead
    my_group, my_lead = me // lead, lax.rem(me, lead)
    bf, f32 = jnp.bfloat16, jnp.float32

    grid_copy = pltpu.make_async_copy(grid_in, grid_ref, grid_sem)
    grid_copy.start()
    barrier = pltpu.get_barrier_semaphore()
    pl.semaphore_signal(barrier, inc=1, device_id={"gy": peer})

    @pl.loop(1, gx)
    def _(t):
        pl.semaphore_signal(barrier, inc=1, device_id={"gx": lax.rem(me + t, gx)})

    def frows(f):
        return pl.ds(al(f * x_local, x_local), x_local)

    def blk(j):
        return pl.ds(al(j * x_local, x_local), x_local)

    def lanes(base, g):
        return pl.ds(al(base + g * cols, cols), cols)

    make_table(ycode_ref, half * y_ref.shape[0], NY, y_ref, ta, tb, fc, fs)
    grid_copy.wait()

    @pl.loop(0, lead)
    def _(t):
        f = lax.rem(my_lead + t, lead)
        other[frows(f), :] = jnp.dot(
            grid_ref[frows(f), :], y_ref[:, pl.ds(al(peer * kpad, kpad), kpad)], preferred_element_type=f32
        ).astype(bf)

    pl.semaphore_wait(barrier, gx)

    def swap(f):
        return pltpu.make_async_remote_copy(
            src_ref=other.at[frows(f), :], dst_ref=inc.at[frows(f), :], send_sem=gs.at[f], recv_sem=gr.at[f],
            device_id={"gy": peer})

    @pl.loop(0, lead)
    def _(t):
        swap(lax.rem(my_lead + t, lead)).start()

    def out1(j):
        f, g = lax.rem(j, lead), j // lead
        return pltpu.make_async_remote_copy(
            src_ref=part.at[frows(f), lanes(0, g)], dst_ref=lines.at[blk(me), :], send_sem=s1.at[j],
            recv_sem=r1.at[me], device_id={"gx": j})

    def in1(j):
        return pltpu.make_async_remote_copy(
            src_ref=part.at[frows(0), lanes(0, 0)], dst_ref=lines.at[blk(j), :], send_sem=s1.at[j],
            recv_sem=r1.at[j], device_id={"gx": j})

    @pl.loop(0, lead)
    def _(t):
        f = lax.rem(my_lead + t, lead)
        own = jnp.dot(
            grid_ref[frows(f), :], y_ref[:, pl.ds(al(half * kpad, kpad), kpad)], preferred_element_type=f32
        )
        swap(f).wait_recv()
        part[frows(f), :] = (own + inc[frows(f), :].astype(f32)).astype(bf)

        @pl.loop(0, groups)
        def _(u):
            g = lax.rem(my_group + u, groups)
            j = g * lead + f

            @pl.when(j != me)
            def _():
                out1(j).start()

    lines[blk(me), :] = part[frows(my_lead), lanes(0, my_group)]

    make_table(xcode_ref, 0, NX, xt, ta, tb, fc, fs)
    acc[...] = jnp.zeros_like(acc)

    @pl.loop(0, gx)
    def _(t):
        f = lax.rem(my_lead + lead - t // groups, lead)
        g = lax.rem(my_group + t, groups)
        j = g * lead + f

        @pl.when(j != me)
        def _():
            in1(j).wait_recv()

        acc[...] += jnp.dot(lines[blk(j), :].T, xt[blk(j), :], preferred_element_type=f32)

    coarse[...] = acc[...].T.astype(bf)

    def out2(j):
        return pltpu.make_async_remote_copy(
            src_ref=syn.at[blk(j), :], dst_ref=wide_ref.at[frows(my_lead), lanes(half * kpad, my_group)],
            send_sem=s2.at[j], recv_sem=r2.at[me], device_id={"gx": j})

    def in2(j):
        f, g = lax.rem(j, lead), j // lead
        return pltpu.make_async_remote_copy(
            src_ref=syn.at[blk(j), :], dst_ref=wide_ref.at[frows(f), lanes(half * kpad, g)],
            send_sem=s2.at[j], recv_sem=r2.at[j], device_id={"gx": j})

    def mrows(j):
        return pl.ds(al(j * kx, kx), kx)

    def out3(j):
        return pltpu.make_async_remote_copy(
            src_ref=coarse.at[mrows(j), :], dst_ref=spec_ref.at[mrows(my_lead), lanes(0, my_group)],
            send_sem=s3.at[j], recv_sem=r3.at[me], device_id={"gx": j})

    def in3(j):
        f, g = lax.rem(j, lead), j // lead
        return pltpu.make_async_remote_copy(
            src_ref=coarse.at[mrows(j), :], dst_ref=spec_ref.at[mrows(f), lanes(0, g)],
            send_sem=s3.at[j], recv_sem=r3.at[j], device_id={"gx": j})

    def forward(j, side):
        f, g = lax.rem(j, lead), j // lead
        place = wide_ref.at[frows(f), lanes(side * kpad, g)]
        return pltpu.make_async_remote_copy(
            src_ref=place, dst_ref=place, send_sem=s4.at[j], recv_sem=r4.at[j], device_id={"gy": peer})

    @pl.loop(1, gx)
    def _(t):
        f = lax.rem(my_lead + t // groups, lead)
        g = lax.rem(my_group + t, groups)
        j = g * lead + f
        syn[blk(j), :] = jnp.dot(xt[blk(j), :], coarse[...], preferred_element_type=f32).astype(bf)
        out2(j).start()

    wide_ref[frows(my_lead), lanes(half * kpad, my_group)] = jnp.dot(
        xt[blk(me), :], coarse[...], preferred_element_type=f32
    ).astype(bf)
    spec_ref[mrows(my_lead), lanes(0, my_group)] = coarse[mrows(me), :]

    @pl.loop(1, gx)
    def _(t):
        out3(lax.rem(me + t, gx)).start()

    forward(me, half).start()

    def low_copy(f):
        return pltpu.make_async_copy(low_ref.at[frows(f), :], low_out.at[frows(f), :], low_sem.at[f])

    @pl.loop(0, lead)
    def _(t):
        f = lax.rem(my_lead + lead - t, lead)

        @pl.loop(0, groups)
        def _(u):
            j = lax.rem(my_group + u, groups) * lead + f

            @pl.when(j != me)
            def _():
                in2(j).wait_recv()
                forward(j, half).start()

        @pl.loop(0, groups)
        def _(u):
            forward(u * lead + f, peer).wait_recv()

        low_ref[frows(f), :] = lax.dot_general(
            wide_ref[frows(f), :], y_ref[...], (((1,), (1,)), ((), ())), preferred_element_type=f32
        ).astype(bf)
        low_copy(f).start()

    @pl.loop(1, gx)
    def _(t):
        j = lax.rem(me + t, gx)
        in3(j).wait_recv()
        out1(j).wait_send()
        out2(j).wait_send()
        out3(j).wait_send()

    @pl.loop(0, gx)
    def _(j):
        forward(j, half).wait_send()

    @pl.loop(0, lead)
    def _(f):
        swap(f).wait_send()
        low_copy(f).wait()


def exchange(gx, lead, x_local, kx, kpad, cols, grid, x_codes, y_codes):
    bf, f32 = jnp.bfloat16, jnp.float32
    rows, codes = lead * x_local, gx * kx
    dma = pltpu.SemaphoreType.DMA
    vmem = pl.BlockSpec(memory_space=pltpu.VMEM)
    y_local = grid.shape[1]
    tall = max(gx * x_local, y_local) // STEP
    return pl.pallas_call(
        functools.partial(exchange_kernel, gx, lead, x_local, kx, kpad, cols),
        out_shape=(
            jax.ShapeDtypeStruct((lead * kx, kpad), bf),
            jax.ShapeDtypeStruct((rows, y_local), bf),
        ),
        in_specs=[pl.BlockSpec(memory_space=pl.ANY), vmem, vmem],
        out_specs=(vmem, pl.BlockSpec(memory_space=pl.ANY)),
        scratch_shapes=[
            pltpu.VMEM((rows, y_local), bf),
            pltpu.VMEM((rows, 2 * kpad), bf),
            pltpu.VMEM((rows, y_local), bf),
            pltpu.VMEM((y_local, 2 * kpad), bf),
            pltpu.VMEM((tall, codes), f32),
            pltpu.VMEM((tall, codes), f32),
            pltpu.VMEM((STEP, codes), f32),
            pltpu.VMEM((STEP, codes), f32),
            pltpu.VMEM((rows, kpad), bf),
            pltpu.VMEM((rows, kpad), bf),
            pltpu.VMEM((rows, kpad), bf),
            pltpu.VMEM((gx * x_local, cols), bf),
            pltpu.VMEM((gx * x_local, codes), bf),
            pltpu.VMEM((cols, codes), f32),
            pltpu.VMEM((codes, cols), bf),
            pltpu.VMEM((gx * x_local, cols), bf),
            dma((lead,)), dma((lead,)),
        ] + [dma((gx,))] * 8 + [dma, dma((lead,))],
        compiler_params=pltpu.CompilerParams(
            collective_id=0, has_side_effects=True, vmem_limit_bytes=60 * 1024 * 1024
        ),
    )(grid, x_codes, y_codes)


def build(gx, gy):
    def local(fields, x_codes, y_codes):
        nf, nz, x_local, y_local = fields.shape
        lead = nf * nz
        ky = y_codes.shape[0] // gy
        kx = x_codes.shape[0] // gx
        unit = 128 * gx // math.gcd(128 * gx, lead)
        if unit > 2 * ky:
            unit = gx // math.gcd(gx, lead)
        kpad = -(-ky // unit) * unit
        cols = lead * kpad // gx
        me_y = lax.axis_index("gy")
        y_first = me_y * y_local
        padded = jnp.pad(y_codes.reshape(gy, ky), ((0, 0), (0, kpad - ky)))
        live = jnp.broadcast_to(jnp.arange(kpad)[None] < ky, (gy, kpad)).reshape(-1)
        grid = fields.reshape(lead * x_local, y_local)
        if gy == 2 and cols % 128 == 0 and cols <= kpad and kpad // cols == gx // lead and x_local % (8 * STEP // gx) == 0 and y_local % (8 * STEP) == 0 and kx % 16 == 0 and gx * kx == gy * kpad:
            padded = jnp.pad(y_codes.reshape(gy, ky), ((0, 0), (0, kpad - ky)), constant_values=-1)
            spec, low = exchange(
                gx, lead, x_local, kx, kpad, cols, grid, x_codes.reshape(1, -1), padded.reshape(1, -1)
            )
            low = low.astype(jnp.float32)
            spectrum = spec.astype(jnp.float32)[:, :ky].reshape(nf, nz, kx, ky)
            return spectrum, low.reshape(nf, nz, x_local, y_local)
        x_tab = mode_table(x_codes, 0, x_local * gx, NX)
        y_tab = mode_table(padded.reshape(-1), y_first, y_local, NY, live)
        part = jnp.dot(grid, y_tab, preferred_element_type=jnp.float32).reshape(lead * x_local, gy, kpad)
        own = lax.dynamic_index_in_dim(part, me_y, 1, keepdims=False)
        for shift in range(1, gy):
            there = lax.rem(me_y + shift, gy)
            block = lax.dynamic_index_in_dim(part, there, 1, keepdims=False).astype(jnp.bfloat16)
            got = lax.ppermute(block, "gy", [(i, (i + shift) % gy) for i in range(gy)])
            own = own + got.astype(jnp.float32)
        send = own.astype(jnp.bfloat16).reshape(lead, x_local, kpad)
        if cols <= kpad:
            def spread(a):
                n = a.shape[1]
                return a.reshape(lead, n, kpad // cols, cols).transpose(0, 2, 1, 3).reshape(gx, n, cols)

            def merge(a):
                n = a.shape[1]
                return a.reshape(lead, kpad // cols, n, cols).transpose(0, 2, 1, 3).reshape(lead, n, kpad)
        else:
            def spread(a):
                n = a.shape[1]
                return a.transpose(1, 0, 2).reshape(n, gx, cols).transpose(1, 0, 2)

            def merge(a):
                n = a.shape[1]
                return a.transpose(1, 0, 2).reshape(n, lead, kpad).transpose(1, 0, 2)
        lines = lax.all_to_all(spread(send), "gx", split_axis=0, concat_axis=0, tiled=True)
        lines = lines.reshape(gx * x_local, cols)
        modes = lax.dot_general(x_tab, lines, (((0,), (0,)), ((), ())), preferred_element_type=jnp.float32)
        coarse = modes.astype(jnp.bfloat16)
        synth = jnp.dot(x_tab, coarse, preferred_element_type=jnp.float32).astype(jnp.bfloat16)
        back = lax.all_to_all(synth.reshape(gx, x_local, cols), "gx", split_axis=0, concat_axis=0, tiled=True)
        spec = lax.all_to_all(coarse.reshape(gx, kx, cols), "gx", split_axis=0, concat_axis=0, tiled=True)
        spectrum = merge(spec)[:, :, :ky].astype(jnp.float32).reshape(nf, nz, kx, ky)
        mine = merge(back).reshape(lead * x_local, kpad)
        y_parts = y_tab.reshape(y_local, gy, kpad)
        whole = jnp.zeros((gy, lead * x_local, kpad), jnp.bfloat16)
        whole = lax.dynamic_update_index_in_dim(whole, mine, me_y, 0)
        for shift in range(1, gy):
            got = lax.ppermute(mine, "gy", [(i, (i + shift) % gy) for i in range(gy)])
            whole = lax.dynamic_update_index_in_dim(whole, got, lax.rem(me_y + gy - shift, gy), 0)
        wide = whole.transpose(1, 0, 2).reshape(lead * x_local, gy * kpad)
        low = lax.dot_general(wide, y_tab, (((1,), (1,)), ((), ())), preferred_element_type=jnp.float32)
        return spectrum, low.reshape(nf, nz, x_local, y_local)

    return local


def solution(mesh):
    return jax.shard_map(
        build(mesh.shape["gx"], mesh.shape["gy"]),
        mesh=mesh,
        in_specs=(P(None, None, "gx", "gy"), P(), P()),
        out_specs=(P(None, None, "gx", "gy"), P(None, None, "gx", "gy")),
        check_vma=False,
    )
```

profile of v0, /device:TPU:0, one launch (start us, length us, event | category | flops | bytes accessed | tf_op | source)
XLA Modules:
  0.0 61.8 jit_solution(9767326592186261480)
XLA Ops:
  0.6 0.8 %reshape.30 = s32[2,510]{1,0:T(2,128)S(1)} reshape(s32[1020]{0:T(1024)} %param.5) | data formatting | bytes 8160 | tf_op jit(solution)/shard_map/reshape | solution.py:342
  1.4 0.6 copy.7
  2.0 54.4 %shard_map.50 = (bf16[256,512]{1,0:T(8,128)(2,1)}, bf16[768,1536]{1,0:T(8,128)(2,1)}) custom-call(bf16[768,1536]{1,0:T(8,128)(2,1)} %bitcast.18, s32[1,1024]{1,0:T(1,128)} %bitcast.21, s32[1,1024]{1,0:T(1,128)} %bitcast.20), custom_call_target="tpu_custom_call" | custom-call | tf_op jit(solution)/shard_map/pallas_call | solution.py:292
  56.4 0.0 copy-start
  56.4 4.5 %convert.6 = f32[4,1,192,1536]{3,2,1,0:T(8,128)} convert(bf16[4,1,192,1536]{3,2,1,0:T(8,128)(2,1)} %bitcast.17) | non-fusion elementwise | flops 1179648 | bytes 7077888
  60.9 0.0 copy-done
  60.9 0.9 %convert.4 = f32[4,1,64,510]{3,2,1,0:T(8,128)} convert(bf16[4,1,64,510]{3,2,1,0:T(8,128)(2,1)S(1)} %bitcast.19) | non-fusion elementwise | flops 130560 | bytes 783360
  (1 shorter events, 0.0 us)
Async XLA Ops:
  56.4 4.5 %copy-start = (bf16[256,512]{1,0:T(8,128)(2,1)S(1)}, bf16[256,512]{1,0:T(8,128)(2,1)}, u32[]{:S(2)}) copy-start(bf16[256,512]{1,0:T(8,128)(2,1)} %get-tuple-element.4) | copy-start | bytes 786436
where the time goes:
time: 63 us; the launch traced here: 61.8 us
  Pallas kernels  54.4 us (86%)
  other arithmetic  5.39 us (9%)
  local copies, waits for them, and re-layouts  1.38 us (2%)
  between operations  0.65 us (1%)
    pallas_call x1, Pallas kernels, exchange(): pl.pallas_call(functools.partial(exchange_kernel, gx, lead, x_local, kx,...  54.4 us
    unnamed x2, other arithmetic  5.39 us

commit v1 on v0

v1 whole, which is shorter than its diff:
```python
import functools
import math

import jax
import jax.numpy as jnp
from jax import lax
from jax.experimental import pallas as pl
from jax.experimental.pallas import tpu as pltpu
from jax.sharding import PartitionSpec as P

NX = 3072
NY = 3072
BAND = 512
STEP = 64


def angle(freq, position, length):
    phase = freq[None, :] * position[:, None] % length
    return phase.astype(jnp.float32) * (2.0 * math.pi / length)


def mode_parts(picked, first, amount, length, live=None):
    step = 64 if amount % 64 == 0 else 8
    freq = jnp.where(picked <= BAND, picked, picked - BAND)
    coarse_angle = angle(freq, first + step * jnp.arange(amount // step, dtype=jnp.int32), length)
    fine_angle = angle(freq, jnp.arange(step, dtype=jnp.int32), length)
    norm = jnp.where(picked == 0, 1.0 / math.sqrt(length), math.sqrt(2.0 / length)).astype(jnp.float32)
    if live is not None:
        norm = jnp.where(live, norm, 0.0)
    is_cos = (picked <= BAND)[None, :]
    c, s = jnp.cos(coarse_angle), jnp.sin(coarse_angle)
    first_part = jnp.where(is_cos, c, s) * norm[None, :]
    second_part = jnp.where(is_cos, -s, c) * norm[None, :]
    fc, fs = jnp.cos(fine_angle), jnp.sin(fine_angle)
    return lax.optimization_barrier((first_part, second_part, fc, fs))


def mode_table(picked, first, amount, length, live=None):
    first_part, second_part, fc, fs = mode_parts(picked, first, amount, length, live)
    table = first_part[:, None, :] * fc[None] + second_part[:, None, :] * fs[None]
    return table.astype(jnp.bfloat16).reshape(amount, picked.shape[0])


def al(v, m):
    return pl.multiple_of(v, m)


def turn(freq, position, shift, length):
    product = freq * position
    quarter = jnp.floor(product * (4.0 / length) + 0.5)
    x = (product * 4.0 - quarter * length) * (2.0 * math.pi / (4 * length))
    x2 = x * x
    s = x + x * x2 * (-1 / 6 + x2 * (1 / 120 + x2 * (-1 / 5040 + x2 * (1 / 362880))))
    c = 1.0 + x2 * (-0.5 + x2 * (1 / 24 + x2 * (-1 / 720 + x2 * (1 / 40320))))
    quarter = quarter - shift
    q = quarter - 4.0 * jnp.floor(quarter * 0.25)
    odd = (q == 1.0) | (q == 3.0)
    cos_value, sin_value = jnp.where(odd, s, c), jnp.where(odd, c, s)
    cos_value = jnp.where((q == 1.0) | (q == 2.0), -cos_value, cos_value)
    return cos_value, jnp.where(q >= 2.0, -sin_value, sin_value)


LANES = 128


def make_table(code, first, length, table, ta, tb, fc, fs):
    amount, codes = table.shape
    f32 = jnp.float32
    freq = jnp.where(code <= BAND, code, code - BAND).astype(f32)
    shift = jnp.where(code <= BAND, 0, 1).astype(f32)
    norm = jnp.where(code == 0, 1.0 / math.sqrt(length), math.sqrt(2.0 / length)).astype(f32)
    norm = jnp.where(code < 0, 0.0, norm)
    row = lax.broadcasted_iota(jnp.int32, (8, codes), 0)

    @pl.loop(0, amount // STEP // 8)
    def _(i):
        c, s = turn(freq, (first + (row + i * 8) * STEP).astype(f32), shift, length)
        ta[pl.ds(al(i * 8, 8), 8), :] = c * norm
        tb[pl.ds(al(i * 8, 8), 8), :] = s * norm

    @pl.loop(0, STEP // 8)
    def _(i):
        c, s = turn(freq, (row + i * 8).astype(f32), 0.0, length)
        fc[pl.ds(al(i * 8, 8), 8), :] = c
        fs[pl.ds(al(i * 8, 8), 8), :] = s

    @pl.loop(0, amount // STEP)
    def _(h):
        table[pl.ds(al(h * STEP, STEP), STEP), :] = (
            ta[pl.ds(h, 1), :] * fc[...] - tb[pl.ds(h, 1), :] * fs[...]
        ).astype(jnp.bfloat16)


def filter_kernel(
    lead, x_local, kx, ky, kpad,
    grid_in, code_in, spec_ref, low_ref,
    grid_ref, code_ref, y_raw, y_codes, y_ref, yta, ytb, yfc, yfs, own, other, inc, part, lines, turned, xt, xta, xtb, xfc, xfs,
    s_own, s_out, s_in, coarse, blocks, wide,
    gs, gr, s1, r1, s2, r2, s3, r3, s4, r4, in_sem,
):
    me = lax.axis_index("gx")
    half = lax.axis_index("gy")
    peer = 1 - half
    bf, f32 = jnp.bfloat16, jnp.float32
    scope = jax.named_scope
    chunks = kpad // LANES
    members = 2 * lead
    modes = xt.shape[1]
    pieces = r2.shape[0] // chunks
    piece = modes // pieces
    rows = lead * x_local
    block = x_local + kx
    plane, spot = me // lead, lax.rem(me, lead)
    side = plane // 2
    base = side * members
    mine = me - base
    hub_in, end_in = 1 - side, side
    hub_base = base + hub_in * lead
    is_hub = plane == 1 + side
    across = (2 - side) * lead + spot

    grid_copy = pltpu.make_async_copy(grid_in, grid_ref, in_sem.at[0])
    code_copy = pltpu.make_async_copy(code_in, code_ref, in_sem.at[1])
    code_copy.start()
    grid_copy.start()
    barrier = pltpu.get_barrier_semaphore()
    pl.semaphore_signal(barrier, inc=1, device_id={"gy": peer})

    @pl.loop(1, members)
    def _(t):
        pl.semaphore_signal(barrier, inc=1, device_id={"gx": base + lax.rem(mine + t, members)})

    @pl.when(is_hub)
    def _():
        pl.semaphore_signal(barrier, inc=1, device_id={"gx": across})

    def span(i, n):
        return pl.ds(al(i * n, n), n)

    def swap(k):
        return pltpu.make_async_remote_copy(
            src_ref=other.at[k], dst_ref=inc.at[k], send_sem=gs, recv_sem=gr.at[k], device_id={"gy": peer})

    def up(k, f):
        return pltpu.make_async_remote_copy(
            src_ref=part.at[k, span(f, x_local), :], dst_ref=lines.at[k, span(mine, x_local), :],
            send_sem=s1, recv_sem=r1.at[k], device_id={"gx": hub_base + f})

    def up_in(k):
        taken = lines.at[k, pl.ds(0, (members - 1) * x_local), :]
        return pltpu.make_async_remote_copy(
            src_ref=taken, dst_ref=taken, send_sem=s1, recv_sem=r1.at[k], device_id={"gx": hub_base})

    def sent(view, sem):
        pltpu.make_async_remote_copy(
            src_ref=view, dst_ref=view, send_sem=sem, recv_sem=gr.at[0], device_id={"gy": peer}).wait_send()

    def cross(k, m):
        return pltpu.make_async_remote_copy(
            src_ref=s_out.at[k, span(m, piece), :], dst_ref=s_in.at[k, span(m, piece), :],
            send_sem=s2, recv_sem=r2.at[k * pieces + m], device_id={"gx": across})

    def down(k, b):
        return pltpu.make_async_remote_copy(
            src_ref=blocks.at[k, b], dst_ref=wide.at[k, spot, :, span(half, LANES)],
            send_sem=s3, recv_sem=r3.at[k * lead + spot], device_id={"gx": base + b})

    def down_in(k, f):
        return pltpu.make_async_remote_copy(
            src_ref=blocks.at[k, 0], dst_ref=wide.at[k, f, :, span(half, LANES)],
            send_sem=s3, recv_sem=r3.at[k * lead + f], device_id={"gx": hub_base + f})

    def forward(k, f, who):
        place = wide.at[k, f, pl.ds(0, x_local), span(who, LANES)]
        return pltpu.make_async_remote_copy(
            src_ref=place, dst_ref=place, send_sem=s4, recv_sem=r4.at[k * lead + f],
            device_id={"gy": peer})

    def local(f):
        return is_hub & (f == spot)

    width = chunks * LANES * 2
    y_raw[...] = jnp.full(y_raw.shape, -1, jnp.int32)
    with scope("codewait"):
        code_copy.wait()
    y_raw[:, : 2 * ky] = code_ref[:, modes:]
    first_half = jnp.broadcast_to(y_raw[...], (8, width))
    second_half = pltpu.roll(first_half, width - ky, 1)
    live = lax.broadcasted_iota(jnp.int32, (8, width), 1) < ky
    first_half = jnp.where(live, first_half, -1)
    second_half = jnp.where(live, second_half, -1)
    for k in range(chunks):
        y_codes[k, :, :LANES] = first_half[:, k * LANES : (k + 1) * LANES]
        y_codes[k, :, LANES:] = second_half[:, k * LANES : (k + 1) * LANES]

    def y_table(k):
        with scope("ytab"):
            make_table(y_codes[k, :1, :], half * y_ref.shape[1], NY, y_ref.at[k], yta, ytb, yfc, yfs)

    def sums(k):
        if k == 0:
            with scope("gridwait"):
                grid_copy.wait()
        with scope("dotA"):
            both = jnp.dot(grid_ref[...], y_ref[k], preferred_element_type=f32)
            low_part, high_part = both[:, :LANES], both[:, LANES:]
            other[k] = jnp.where(half == 0, high_part, low_part).astype(bf)
            own[k] = jnp.where(half == 0, low_part, high_part)
        if k == 0:
            with scope("barrier"):
                pl.semaphore_wait(barrier, members + jnp.where(is_hub, 1, 0))
        swap(k).start()

    def rise(k):
        with scope("swapwait"):
            swap(k).wait_recv()
        part[k] = (own[k] + inc[k].astype(f32)).astype(bf)

        @pl.loop(0, lead)
        def _(t):
            f = lax.rem(spot + t, lead)

            @pl.when(jnp.logical_not(local(f)))
            def _():
                up(k, f).start()

        @pl.when(is_hub)
        def _():
            lines[k, span(mine, x_local), :] = part[k, span(spot, x_local), :]

    def partial_sum(k):
        with scope("upwait"):
            up_in(k).wait_recv()

        with scope("dotB"):
            turned[...] = lines[k].T

            @pl.loop(0, pieces)
            def _(m):
                got = jnp.dot(turned[...], xt[:, span(m, piece)], preferred_element_type=f32).T
                s_own[k, span(m, piece), :] = got
                s_out[k, span(m, piece), :] = got.astype(bf)
                cross(k, m).start()

    def whole_sum(k):
        @pl.loop(0, pieces)
        def _(m):
            with scope("crosswait"):
                cross(k, m).wait_recv()
            coarse[k, span(m, piece), :] = (
                s_own[k, span(m, piece), :] + s_in[k, span(m, piece), :].astype(f32)
            ).astype(bf)

        for place in (end_in, hub_in):
            with scope("dotC"):
                syn = jnp.dot(xt[span(place, rows), :], coarse[k], preferred_element_type=f32).astype(bf)
                blocks[k, span(place, lead), :x_local, :] = syn.reshape(lead, x_local, LANES)
                blocks[k, span(place, lead), x_local:, :] = coarse[
                    k, span(base // lead + place, lead * kx), :
                ].reshape(lead, kx, LANES)

            @pl.loop(1, lead + 1)
            def _(t):
                b = place * lead + lax.rem(spot + t, lead)

                @pl.when(b != mine)
                def _():
                    down(k, b).start()

        wide[k, spot, :, span(half, LANES)] = blocks[k, mine]

    def take(k):
        @pl.loop(1, lead + 1)
        def _(t):
            f = lax.rem(spot + lead - lax.rem(t, lead), lead)

            @pl.when(jnp.logical_not(local(f)))
            def _():
                with scope("downwait"):
                    down_in(k, f).wait_recv()

            forward(k, f, half).start()
            found = wide[k, f, pl.ds(x_local, kx), span(half, LANES)].astype(f32)
            spec_ref[span(f, kx), pl.ds(k * LANES, min(LANES, ky - k * LANES))] = found[:, : ky - k * LANES]

    def expand(k):
        @pl.loop(1, lead + 1)
        def _(t):
            f = lax.rem(spot + lead - lax.rem(t, lead), lead)
            with scope("fwdwait"):
                forward(k, f, peer).wait_recv()
            with scope("dotD"):
                got = lax.dot_general(
                    wide[k, f, :x_local, :], y_ref[k], (((1,), (1,)), ((), ())), preferred_element_type=f32)
                if k > 0:
                    got = got + low_ref[span(f, x_local), :]
                low_ref[span(f, x_local), :] = got

    y_table(0)
    sums(0)
    y_table(1)

    @pl.when(half == 0)
    def _():
        rise(0)

    sums(1)

    @pl.when(half == 1)
    def _():
        rise(0)

    if chunks > 2:
        y_table(2)
    rise(1)

    def late_sums(k):
        sums(k)
        if k + 1 < chunks:
            y_table(k + 1)
        rise(k)

    @pl.when(is_hub)
    def _():
        with scope("xtab"):
            make_table(code_ref[:, :modes], side * xt.shape[0], NX, xt, xta, xtb, xfc, xfs)
        for k in range(chunks):
            partial_sum(k)
            if k + 2 < chunks:
                late_sums(k + 2)
            if 0 < k < chunks - 1:
                whole_sum(k - 1)
        take(0)
        expand(0)
        for k in range(max(chunks - 2, 0), chunks):
            whole_sum(k)
        for k in range(1, chunks):
            take(k)
            expand(k)

    @pl.when(jnp.logical_not(is_hub))
    def _():
        for k in range(2, chunks):
            late_sums(k)
        for k in range(chunks):
            take(k)
            expand(k)

    with scope("drain"):
        sent(other, gs)
        sent(wide.at[:, :, pl.ds(0, x_local), pl.ds(0, LANES)], s4)

        @pl.when(is_hub)
        def _():
            sent(part.at[:, pl.ds(0, rows - x_local), :], s1)
            sent(s_out, s2)
            sent(blocks.at[:, pl.ds(0, members - 1)], s3)

        @pl.when(jnp.logical_not(is_hub))
        def _():
            sent(part, s1)


def spectral_filter(lead, x_local, kx, ky, kpad, grid, codes):
    bf, f32 = jnp.bfloat16, jnp.float32
    y_local = grid.shape[1]
    rows, members, modes = lead * x_local, 2 * lead, codes.shape[1] - 2 * ky
    chunks, pieces = kpad // LANES, 4
    tall_x, tall_y = members * x_local // STEP, y_local // STEP
    block = x_local + kx
    dma = pltpu.SemaphoreType.DMA
    vmem = pl.BlockSpec(memory_space=pltpu.VMEM)
    return pl.pallas_call(
        functools.partial(filter_kernel, lead, x_local, kx, ky, kpad),
        out_shape=(
            jax.ShapeDtypeStruct((lead * kx, ky), f32),
            jax.ShapeDtypeStruct((rows, y_local), f32),
        ),
        in_specs=[pl.BlockSpec(memory_space=pl.ANY)] * 2,
        out_specs=(vmem, vmem),
        scratch_shapes=[
            pltpu.VMEM((rows, y_local), bf),
            pltpu.VMEM(codes.shape, jnp.int32),
            pltpu.VMEM((1, 2 * kpad), jnp.int32),
            pltpu.VMEM((chunks, 8, 2 * LANES), jnp.int32),
            pltpu.VMEM((chunks, y_local, 2 * LANES), bf),
            pltpu.VMEM((tall_y, 2 * LANES), f32),
            pltpu.VMEM((tall_y, 2 * LANES), f32),
            pltpu.VMEM((STEP, 2 * LANES), f32),
            pltpu.VMEM((STEP, 2 * LANES), f32),
            pltpu.VMEM((chunks, rows, LANES), f32),
            pltpu.VMEM((chunks, rows, LANES), bf),
            pltpu.VMEM((chunks, rows, LANES), bf),
            pltpu.VMEM((chunks, rows, LANES), bf),
            pltpu.VMEM((chunks, members * x_local, LANES), bf),
            pltpu.VMEM((LANES, members * x_local), bf),
            pltpu.VMEM((members * x_local, modes), bf),
            pltpu.VMEM((tall_x, modes), f32),
            pltpu.VMEM((tall_x, modes), f32),
            pltpu.VMEM((STEP, modes), f32),
            pltpu.VMEM((STEP, modes), f32),
            pltpu.VMEM((chunks, modes, LANES), f32),
            pltpu.VMEM((chunks, modes, LANES), bf),
            pltpu.VMEM((chunks, modes, LANES), bf),
            pltpu.VMEM((chunks, modes, LANES), bf),
            pltpu.VMEM((chunks, members, block, LANES), bf),
            pltpu.VMEM((chunks, lead, block, 2 * LANES), bf),
            dma, dma((chunks,)),
            dma, dma((chunks,)),
            dma, dma((chunks * pieces,)),
            dma, dma((chunks * lead,)),
            dma, dma((chunks * lead,)),
            dma((2,)),
        ],
        compiler_params=pltpu.CompilerParams(
            collective_id=0, has_side_effects=True, vmem_limit_bytes=46 * 1024 * 1024
        ),
    )(grid, codes)


def build(gx, gy):
    def local(fields, x_codes, y_codes):
        nf, nz, x_local, y_local = fields.shape
        lead = nf * nz
        ky = y_codes.shape[0] // gy
        kx = x_codes.shape[0] // gx
        unit = 128 * gx // math.gcd(128 * gx, lead)
        if unit > 2 * ky:
            unit = gx // math.gcd(gx, lead)
        kpad = -(-ky // unit) * unit
        cols = lead * kpad // gx
        me_y = lax.axis_index("gy")
        y_first = me_y * y_local
        grid = fields.reshape(lead * x_local, y_local)
        fits = gy == 2 and gx == 4 * lead and kpad % LANES == 0 and kpad >= 4 * LANES and kx % 16 == 0
        fits = fits and x_local % 16 == 0 and 2 * lead * x_local % (8 * STEP) == 0
        fits = fits and y_local % (8 * STEP) == 0 and gx * kx % (4 * LANES) == 0
        if fits:
            spec, low = spectral_filter(
                lead, x_local, kx, ky, kpad, grid, jnp.concatenate([x_codes, y_codes]).reshape(1, -1))
            return spec.reshape(nf, nz, kx, ky), low.reshape(nf, nz, x_local, y_local)
        padded = jnp.pad(y_codes.reshape(gy, ky), ((0, 0), (0, kpad - ky)))
        live = jnp.broadcast_to(jnp.arange(kpad)[None] < ky, (gy, kpad)).reshape(-1)
        x_tab = mode_table(x_codes, 0, x_local * gx, NX)
        y_tab = mode_table(padded.reshape(-1), y_first, y_local, NY, live)
        part = jnp.dot(grid, y_tab, preferred_element_type=jnp.float32).reshape(lead * x_local, gy, kpad)
        own = lax.dynamic_index_in_dim(part, me_y, 1, keepdims=False)
        for shift in range(1, gy):
            there = lax.rem(me_y + shift, gy)
            block = lax.dynamic_index_in_dim(part, there, 1, keepdims=False).astype(jnp.bfloat16)
            got = lax.ppermute(block, "gy", [(i, (i + shift) % gy) for i in range(gy)])
            own = own + got.astype(jnp.float32)
        send = own.astype(jnp.bfloat16).reshape(lead, x_local, kpad)
        if cols <= kpad:
            def spread(a):
                n = a.shape[1]
                return a.reshape(lead, n, kpad // cols, cols).transpose(0, 2, 1, 3).reshape(gx, n, cols)

            def merge(a):
                n = a.shape[1]
                return a.reshape(lead, kpad // cols, n, cols).transpose(0, 2, 1, 3).reshape(lead, n, kpad)
        else:
            def spread(a):
                n = a.shape[1]
                return a.transpose(1, 0, 2).reshape(n, gx, cols).transpose(1, 0, 2)

            def merge(a):
                n = a.shape[1]
                return a.transpose(1, 0, 2).reshape(n, lead, kpad).transpose(1, 0, 2)
        lines = lax.all_to_all(spread(send), "gx", split_axis=0, concat_axis=0, tiled=True)
        lines = lines.reshape(gx * x_local, cols)
        modes = lax.dot_general(x_tab, lines, (((0,), (0,)), ((), ())), preferred_element_type=jnp.float32)
        coarse = modes.astype(jnp.bfloat16)
        synth = jnp.dot(x_tab, coarse, preferred_element_type=jnp.float32).astype(jnp.bfloat16)
        back = lax.all_to_all(synth.reshape(gx, x_local, cols), "gx", split_axis=0, concat_axis=0, tiled=True)
        spec = lax.all_to_all(coarse.reshape(gx, kx, cols), "gx", split_axis=0, concat_axis=0, tiled=True)
        spectrum = merge(spec)[:, :, :ky].astype(jnp.float32).reshape(nf, nz, kx, ky)
        mine = merge(back).reshape(lead * x_local, kpad)
        y_parts = y_tab.reshape(y_local, gy, kpad)
        whole = jnp.zeros((gy, lead * x_local, kpad), jnp.bfloat16)
        whole = lax.dynamic_update_index_in_dim(whole, mine, me_y, 0)
        for shift in range(1, gy):
            got = lax.ppermute(mine, "gy", [(i, (i + shift) % gy) for i in range(gy)])
            whole = lax.dynamic_update_index_in_dim(whole, got, lax.rem(me_y + gy - shift, gy), 0)
        wide = whole.transpose(1, 0, 2).reshape(lead * x_local, gy * kpad)
        low = lax.dot_general(wide, y_tab, (((1,), (1,)), ((), ())), preferred_element_type=jnp.float32)
        return spectrum, low.reshape(nf, nz, x_local, y_local)

    return local


def solution(mesh):
    return jax.shard_map(
        build(mesh.shape["gx"], mesh.shape["gy"]),
        mesh=mesh,
        in_specs=(P(None, None, "gx", "gy"), P(), P()),
        out_specs=(P(None, None, "gx", "gy"), P(None, None, "gx", "gy")),
        check_vma=False,
    )
```

time: 63 us -> 57.8 us (0.917); the launches traced: 61.8 us -> 57.6 us
  other arithmetic: 5.39 us -> 0.71 us
  local copies, waits for them, and re-layouts: 1.38 us -> 4.65 us
  Pallas kernels: 54.4 us -> 51.6 us
    unnamed x2 -> x0, other arithmetic: 5.39 us -> none
    unnamed x4, local copies, waits for them, and re-layouts: 0.61 us -> 4.65 us
    pallas_call x1, Pallas kernels: 54.4 us -> 51.6 us  [spectral_filter(): pl.pallas_call(functools.partial(filter_kernel, lead, x_local, kx, ky, kp...]
    reshape x1 -> x0, local copies, waits for them, and re-layouts: 0.76 us -> none  [local(): y_codes.reshape(gy, ky)]
    concatenate x0 -> x1, other arithmetic: none -> 0.71 us  [local(): jnp.concatenate([x_codes, y_codes]).reshape(1, -1)]
where the time goes in v1:
time: 57.8 us; the launch traced here: 57.6 us
  Pallas kernels  51.6 us (89%)
  local copies, waits for them, and re-layouts  4.65 us (8%)
  other arithmetic  0.71 us (1%)
  between operations  0.64 us (1%)
    pallas_call x1, Pallas kernels, spectral_filter(): pl.pallas_call(functools.partial(filter_kernel, lead, x_local, kx, ky, kp...  51.6 us
    unnamed x4, local copies, waits for them, and re-layouts  4.65 us

profile of v1, /device:TPU:0, one launch (start us, length us, event | category | flops | bytes accessed | tf_op | source)
XLA Modules:
  0.0 57.6 jit_solution(17096176612492980334)
XLA Ops:
  0.6 0.7 %pad_add_fusion = s32[2044]{0:T(1024)S(1)} fusion(s32[1020]{0:T(1024)} %param.5, s32[1024]{0:T(1024)} %param.4), kind=kLoop, calls=%fused_computation | loop fusion | flops 2044 | bytes 16352 | tf_op jit(solution)/shard_map/concatenate | solution.py:440
  1.3 0.0 copy-start
  1.3 1.7 %copy-done = bf16[4,1,192,1536]{3,2,1,0:T(8,128)(2,1)S(1)} copy-done((bf16[4,1,192,1536]{3,2,1,0:T(8,128)(2,1)S(1)}, bf16[4,1,192,1536]{3,2,1,0:T(8,128)(2,1)}, u32[]{:S(2)}) %copy-start) | copy-done | bytes 2359320
  3.0 51.6 %shard_map.50 = (f32[256,510]{1,0:T(8,128)S(1)}, f32[768,1536]{1,0:T(8,128)S(1)}) custom-call(bf16[768,1536]{1,0:T(8,128)(2,1)S(1)} %bitcast.9, s32[1,2044]{1,0:T(1,128)S(1)} %bitcast.11), custom_call_target="tpu_custom_call" | custom-call | tf_op jit(solution)/shard_map/pallas_call | solution.py:373
  54.6 0.8 %copy.9 = f32[4,1,64,510]{3,2,1,0:T(8,128)} copy(f32[4,1,64,510]{3,2,1,0:T(8,128)S(1)} %bitcast.10) | data formatting | bytes 1044480
  55.4 2.2 %copy.10 = f32[4,1,192,1536]{3,2,1,0:T(8,128)} copy(f32[4,1,192,1536]{3,2,1,0:T(8,128)S(1)} %bitcast.8) | data formatting | bytes 9437184
Async XLA Ops:
  1.3 1.7 %copy-start = (bf16[4,1,192,1536]{3,2,1,0:T(8,128)(2,1)S(1)}, bf16[4,1,192,1536]{3,2,1,0:T(8,128)(2,1)}, u32[]{:S(2)}) copy-start(bf16[4,1,192,1536]{3,2,1,0:T(8,128)(2,1)} %param.3) | copy-start | bytes 7077892

commit v2 on v1

--- a/solution.py
+++ b/solution.py
@@ -91,12 +91,24 @@
         ).astype(jnp.bfloat16)
 
 
+def flipped(spot, t, lead):
+    f = spot
+    for bit in range(lead.bit_length()):
+        if t >> bit & 1:
+            f = f + (1 << bit) - (2 << bit) * lax.rem(f // (1 << bit), 2)
+    return f
+
+
+def near_first(lead):
+    return sorted(range(lead - 1, 0, -1), key=lambda t: bin(t).count("1"))
+
+
 def filter_kernel(
     lead, x_local, kx, ky, kpad,
-    grid_in, code_in, spec_ref, low_ref,
-    grid_ref, code_ref, y_raw, y_codes, y_ref, yta, ytb, yfc, yfs, own, other, inc, part, lines, turned, xt, xta, xtb, xfc, xfs,
-    s_own, s_out, s_in, coarse, blocks, wide,
-    gs, gr, s1, r1, s2, r2, s3, r3, s4, r4, in_sem,
+    grid_in, xcode_in, ycode_in, spec_ref, low_ref, wide_last, y_last,
+    grid_ref, xcode_ref, ycode_ref, y_raw, y_codes, y_ref, yta, ytb, yfc, yfs, own, other, inc, part, lines, turned, xt, xta, xtb, xfc, xfs,
+    s_own, s_out, s_in, coarse, blocks, wide, found,
+    gs, gr, s1, r1, s2, r2, s3, r3, s4, r4, s5, r5, s6, r6, in_sem,
 ):
     me = lax.axis_index("gx")
     half = lax.axis_index("gy")
@@ -109,20 +121,22 @@
     pieces = r2.shape[0] // chunks
     piece = modes // pieces
     rows = lead * x_local
-    block = x_local + kx
     plane, spot = me // lead, lax.rem(me, lead)
     side = plane // 2
     base = side * members
     mine = me - base
-    hub_in, end_in = 1 - side, side
-    hub_base = base + hub_in * lead
+    hub_base = base + (1 - side) * lead
+    end_base = base + side * lead
+    own_base = plane * lead
     is_hub = plane == 1 + side
     across = (2 - side) * lead + spot
 
     grid_copy = pltpu.make_async_copy(grid_in, grid_ref, in_sem.at[0])
-    code_copy = pltpu.make_async_copy(code_in, code_ref, in_sem.at[1])
-    code_copy.start()
+    ycode_copy = pltpu.make_async_copy(ycode_in, ycode_ref, in_sem.at[1])
+    xcode_copy = pltpu.make_async_copy(xcode_in, xcode_ref, in_sem.at[2])
+    ycode_copy.start()
     grid_copy.start()
+    xcode_copy.start()
     barrier = pltpu.get_barrier_semaphore()
     pl.semaphore_signal(barrier, inc=1, device_id={"gy": peer})
 
@@ -134,6 +148,17 @@
     def _():
         pl.semaphore_signal(barrier, inc=1, device_id={"gx": across})
 
+    def mate(t):
+        return flipped(spot, t, lead)
+
+    far_first = near_first(lead)[::-1]
+
+    def wide_at(k):
+        return wide_last if k == chunks - 1 else wide.at[k]
+
+    def y_at(k):
+        return y_last if k == chunks - 1 else y_ref.at[k]
+
     def span(i, n):
         return pl.ds(al(i * n, n), n)
 
@@ -160,18 +185,34 @@
             src_ref=s_out.at[k, span(m, piece), :], dst_ref=s_in.at[k, span(m, piece), :],
             send_sem=s2, recv_sem=r2.at[k * pieces + m], device_id={"gx": across})
 
-    def down(k, b):
-        return pltpu.make_async_remote_copy(
-            src_ref=blocks.at[k, b], dst_ref=wide.at[k, spot, :, span(half, LANES)],
-            send_sem=s3, recv_sem=r3.at[k * lead + spot], device_id={"gx": base + b})
+    def relay(k, m):
+        view = coarse.at[k, span(m, piece), :]
+        return pltpu.make_async_remote_copy(
+            src_ref=view, dst_ref=view, send_sem=s5, recv_sem=r5.at[k * pieces + m],
+            device_id={"gx": end_base + spot})
+
+    def down(k, f):
+        return pltpu.make_async_remote_copy(
+            src_ref=blocks.at[k, f], dst_ref=wide_at(k).at[spot, :, span(half, LANES)],
+            send_sem=s3, recv_sem=r3.at[k * lead + spot], device_id={"gx": own_base + f})
+
+    def show(k, f):
+        return pltpu.make_async_remote_copy(
+            src_ref=coarse.at[k, span(own_base + f, kx), :], dst_ref=found.at[k, spot],
+            send_sem=s6, recv_sem=r6.at[k], device_id={"gx": own_base + f})
+
+    def show_in(k):
+        view = found.at[k, pl.ds(0, lead - 1)]
+        return pltpu.make_async_remote_copy(
+            src_ref=view, dst_ref=view, send_sem=s6, recv_sem=r6.at[k], device_id={"gx": own_base})
 
     def down_in(k, f):
         return pltpu.make_async_remote_copy(
-            src_ref=blocks.at[k, 0], dst_ref=wide.at[k, f, :, span(half, LANES)],
-            send_sem=s3, recv_sem=r3.at[k * lead + f], device_id={"gx": hub_base + f})
+            src_ref=blocks.at[k, 0], dst_ref=wide_at(k).at[f, :, span(half, LANES)],
+            send_sem=s3, recv_sem=r3.at[k * lead + f], device_id={"gx": own_base + f})
 
     def forward(k, f, who):
-        place = wide.at[k, f, pl.ds(0, x_local), span(who, LANES)]
+        place = wide_at(k).at[f, :, span(who, LANES)]
         return pltpu.make_async_remote_copy(
             src_ref=place, dst_ref=place, send_sem=s4, recv_sem=r4.at[k * lead + f],
             device_id={"gy": peer})
@@ -182,8 +223,8 @@
     width = chunks * LANES * 2
     y_raw[...] = jnp.full(y_raw.shape, -1, jnp.int32)
     with scope("codewait"):
-        code_copy.wait()
-    y_raw[:, : 2 * ky] = code_ref[:, modes:]
+        ycode_copy.wait()
+    y_raw[:, : 2 * ky] = ycode_ref[...]
     first_half = jnp.broadcast_to(y_raw[...], (8, width))
     second_half = pltpu.roll(first_half, width - ky, 1)
     live = lax.broadcasted_iota(jnp.int32, (8, width), 1) < ky
@@ -195,14 +236,14 @@
 
     def y_table(k):
         with scope("ytab"):
-            make_table(y_codes[k, :1, :], half * y_ref.shape[1], NY, y_ref.at[k], yta, ytb, yfc, yfs)
+            make_table(y_codes[k, :1, :], half * grid_ref.shape[1], NY, y_at(k), yta, ytb, yfc, yfs)
 
     def sums(k):
         if k == 0:
             with scope("gridwait"):
                 grid_copy.wait()
         with scope("dotA"):
-            both = jnp.dot(grid_ref[...], y_ref[k], preferred_element_type=f32)
+            both = jnp.dot(grid_ref[...], y_at(k)[...], preferred_element_type=f32)
             low_part, high_part = both[:, :LANES], both[:, LANES:]
             other[k] = jnp.where(half == 0, high_part, low_part).astype(bf)
             own[k] = jnp.where(half == 0, low_part, high_part)
@@ -216,19 +257,18 @@
             swap(k).wait_recv()
         part[k] = (own[k] + inc[k].astype(f32)).astype(bf)
 
-        @pl.loop(0, lead)
-        def _(t):
-            f = lax.rem(spot + t, lead)
-
-            @pl.when(jnp.logical_not(local(f)))
-            def _():
-                up(k, f).start()
+        for t in far_first:
+            up(k, mate(t)).start()
+
+        @pl.when(jnp.logical_not(is_hub))
+        def _():
+            up(k, spot).start()
 
         @pl.when(is_hub)
         def _():
             lines[k, span(mine, x_local), :] = part[k, span(spot, x_local), :]
 
-    def partial_sum(k):
+    def partial_sum(k, held=1):
         with scope("upwait"):
             up_in(k).wait_recv()
 
@@ -240,61 +280,110 @@
                 got = jnp.dot(turned[...], xt[:, span(m, piece)], preferred_element_type=f32).T
                 s_own[k, span(m, piece), :] = got
                 s_out[k, span(m, piece), :] = got.astype(bf)
-                cross(k, m).start()
-
-    def whole_sum(k):
-        @pl.loop(0, pieces)
-        def _(m):
-            with scope("crosswait"):
-                cross(k, m).wait_recv()
-            coarse[k, span(m, piece), :] = (
-                s_own[k, span(m, piece), :] + s_in[k, span(m, piece), :].astype(f32)
-            ).astype(bf)
-
-        for place in (end_in, hub_in):
+
+                @pl.when(half <= held)
+                def _():
+                    cross(k, m).start()
+
+    mine_x = span(plane - 2 * side, rows)
+
+    def share(k):
+        for t in far_first:
+            show(k, mate(t)).start()
+        found[k, spot] = coarse[k, span(me, kx), :]
+
+    def absorb(k, m):
+        if m < pieces - 1:
+            @pl.when(plane == m)
+            def _():
+                share(k)
+
+        if k == chunks - 1:
             with scope("dotC"):
-                syn = jnp.dot(xt[span(place, rows), :], coarse[k], preferred_element_type=f32).astype(bf)
-                blocks[k, span(place, lead), :x_local, :] = syn.reshape(lead, x_local, LANES)
-                blocks[k, span(place, lead), x_local:, :] = coarse[
-                    k, span(base // lead + place, lead * kx), :
-                ].reshape(lead, kx, LANES)
-
-            @pl.loop(1, lead + 1)
-            def _(t):
-                b = place * lead + lax.rem(spot + t, lead)
-
-                @pl.when(b != mine)
-                def _():
-                    down(k, b).start()
-
-        wide[k, spot, :, span(half, LANES)] = blocks[k, mine]
+                got = jnp.dot(
+                    xt[mine_x, pl.ds(m * piece, piece)], coarse[k, pl.ds(m * piece, piece), :],
+                    preferred_element_type=f32)
+                own[0] = got if m == 0 else own[0] + got
+
+    def meet(k, m):
+        with scope("crosswait"):
+            cross(k, m).wait_recv()
+        part_of = pl.ds(m * piece, piece)
+        coarse[k, part_of, :] = (s_own[k, part_of, :] + s_in[k, part_of, :].astype(f32)).astype(bf)
+        relay(k, m).start()
+        absorb(k, m)
+
+    def receive(k, m):
+        with scope("relaywait"):
+            relay(k, m).wait_recv()
+        absorb(k, m)
+
+    def synthesis(k):
+        if k < chunks - 1:
+            with scope("dotC"):
+                syn = jnp.dot(xt[mine_x, :], coarse[k], preferred_element_type=f32)
+        else:
+            syn = own[0]
+        blocks[k] = syn.astype(bf).reshape(lead, x_local, LANES)
+
+        for t in far_first:
+            down(k, mate(t)).start()
+
+        wide_at(k)[spot, :, span(half, LANES)] = blocks[k, spot]
+
+        @pl.when(plane == pieces - 1)
+        def _():
+            share(k)
+
+    def pass_on(k, f):
+        @pl.when(f != spot)
+        def _():
+            with scope("downwait"):
+                down_in(k, f).wait_recv()
+
+        forward(k, f, half).start()
+
+    def reveal(k):
+        with scope("showwait"):
+            show_in(k).wait_recv()
+        columns = min(LANES, ky - k * LANES)
+        spec_ref[:, pl.ds(k * LANES, columns)] = (
+            found[k].reshape(lead * kx, LANES)[:, :columns].astype(f32))
+
+    def add_field(k, f):
+        with scope("fwdwait"):
+            forward(k, f, peer).wait_recv()
+        with scope("dotD"):
+            got = lax.dot_general(
+                wide_at(k)[f], y_at(k)[...], (((1,), (1,)), ((), ())), preferred_element_type=f32)
+            if k > 0:
+                got = got + low_ref[span(f, x_local), :]
+            low_ref[span(f, x_local), :] = got
+
+    def turn_of(t):
+        return lax.rem(spot + lead - lax.rem(t, lead), lead)
 
     def take(k):
         @pl.loop(1, lead + 1)
         def _(t):
-            f = lax.rem(spot + lead - lax.rem(t, lead), lead)
-
-            @pl.when(jnp.logical_not(local(f)))
-            def _():
-                with scope("downwait"):
-                    down_in(k, f).wait_recv()
-
-            forward(k, f, half).start()
-            found = wide[k, f, pl.ds(x_local, kx), span(half, LANES)].astype(f32)
-            spec_ref[span(f, kx), pl.ds(k * LANES, min(LANES, ky - k * LANES))] = found[:, : ky - k * LANES]
+            pass_on(k, turn_of(t))
+
+        reveal(k)
 
     def expand(k):
         @pl.loop(1, lead + 1)
         def _(t):
-            f = lax.rem(spot + lead - lax.rem(t, lead), lead)
-            with scope("fwdwait"):
-                forward(k, f, peer).wait_recv()
-            with scope("dotD"):
-                got = lax.dot_general(
-                    wide[k, f, :x_local, :], y_ref[k], (((1,), (1,)), ((), ())), preferred_element_type=f32)
-                if k > 0:
-                    got = got + low_ref[span(f, x_local), :]
-                low_ref[span(f, x_local), :] = got
+            add_field(k, turn_of(t))
+
+    def finish():
+        k = chunks - 1
+        add_field(k, spot)
+        for t in reversed(far_first):
+            pass_on(k, mate(t))
+        reveal(k)
+        with scope("fwdwait"):
+            for t in reversed(far_first):
+                forward(k, mate(t), peer).wait_recv()
 
     y_table(0)
     sums(0)
@@ -305,69 +394,106 @@
         rise(0)
 
     sums(1)
+    y_table(2)
 
     @pl.when(half == 1)
     def _():
         rise(0)
 
-    if chunks > 2:
-        y_table(2)
-    rise(1)
-
-    def late_sums(k):
-        sums(k)
-        if k + 1 < chunks:
-            y_table(k + 1)
-        rise(k)
+    def x_table():
+        with scope("xtab"):
+            xcode_copy.wait()
+            make_table(xcode_ref[...], side * xt.shape[0], NX, xt, xta, xtb, xfc, xfs)
 
     @pl.when(is_hub)
     def _():
-        with scope("xtab"):
-            make_table(code_ref[:, :modes], side * xt.shape[0], NX, xt, xta, xtb, xfc, xfs)
+        x_table()
+        rise(1)
+        sums(2)
+        y_table(3)
+
+        @pl.when(half == 1)
+        def _():
+            sums(3)
+
+        partial_sum(0)
+
+        @pl.when(half == 0)
+        def _():
+            sums(3)
+
+        rise(2)
+        rise(3)
+        partial_sum(1)
         for k in range(chunks):
-            partial_sum(k)
+            ahead = pieces - 1 - k
+            for m in range(ahead):
+                meet(k, m)
             if k + 2 < chunks:
-                late_sums(k + 2)
-            if 0 < k < chunks - 1:
-                whole_sum(k - 1)
-        take(0)
-        expand(0)
-        for k in range(max(chunks - 2, 0), chunks):
-            whole_sum(k)
-        for k in range(1, chunks):
+                partial_sum(k + 2, 0 if k + 3 == chunks else 1)
+            for m in range(ahead, pieces):
+                meet(k, m)
+            synthesis(k)
+            if k == chunks - 2:
+                @pl.when(half == 1)
+                def _():
+                    @pl.loop(0, pieces)
+                    def _(m):
+                        cross(chunks - 1, m).start()
+
+        forward(chunks - 1, spot, half).start()
+        for k in range(chunks - 1):
             take(k)
             expand(k)
+        finish()
 
     @pl.when(jnp.logical_not(is_hub))
     def _():
-        for k in range(2, chunks):
-            late_sums(k)
+        sums(2)
+        y_table(3)
+
+        rise(1)
+        sums(3)
+        rise(2)
+        rise(3)
+        x_table()
         for k in range(chunks):
-            take(k)
-            expand(k)
+            for m in range(pieces):
+                receive(k, m)
+            synthesis(k)
+            if k == chunks - 1:
+                forward(k, spot, half).start()
+            if k > 0:
+                take(k - 1)
+                expand(k - 1)
+        finish()
 
     with scope("drain"):
         sent(other, gs)
-        sent(wide.at[:, :, pl.ds(0, x_local), pl.ds(0, LANES)], s4)
+        sent(wide.at[:, :, :, pl.ds(0, LANES)], s4)
+        sent(wide_last.at[:, :, pl.ds(0, LANES)], s4)
+        sent(found.at[:, pl.ds(0, lead - 1)], s6)
+        sent(blocks.at[:, pl.ds(0, lead - 1)], s3)
 
         @pl.when(is_hub)
         def _():
             sent(part.at[:, pl.ds(0, rows - x_local), :], s1)
             sent(s_out, s2)
-            sent(blocks.at[:, pl.ds(0, members - 1)], s3)
+            sent(coarse, s5)
 
         @pl.when(jnp.logical_not(is_hub))
         def _():
             sent(part, s1)
 
 
-def spectral_filter(lead, x_local, kx, ky, kpad, grid, codes):
+def spectral_filter(lead, x_local, kx, ky, kpad, *operands):
     bf, f32 = jnp.bfloat16, jnp.float32
+    operands = [pltpu.with_memory_space_constraint(a, pltpu.HBM) for a in operands]
+    grid, x_codes, y_codes = operands
     y_local = grid.shape[1]
-    rows, members, modes = lead * x_local, 2 * lead, codes.shape[1] - 2 * ky
+    rows, members, modes = lead * x_local, 2 * lead, x_codes.shape[1]
     chunks, pieces = kpad // LANES, 4
     tall_x, tall_y = members * x_local // STEP, y_local // STEP
-    block = x_local + kx
     dma = pltpu.SemaphoreType.DMA
     vmem = pl.BlockSpec(memory_space=pltpu.VMEM)
     return pl.pallas_call(
@@ -375,15 +501,18 @@
         out_shape=(
             jax.ShapeDtypeStruct((lead * kx, ky), f32),
             jax.ShapeDtypeStruct((rows, y_local), f32),
+            jax.ShapeDtypeStruct((lead, x_local, 2 * LANES), bf),
+            jax.ShapeDtypeStruct((y_local, 2 * LANES), bf),
         ),
-        in_specs=[pl.BlockSpec(memory_space=pl.ANY)] * 2,
-        out_specs=(vmem, vmem),
+        in_specs=[pl.BlockSpec(memory_space=pltpu.HBM)] * 3,
+        out_specs=(vmem,) * 4,
         scratch_shapes=[
             pltpu.VMEM((rows, y_local), bf),
-            pltpu.VMEM(codes.shape, jnp.int32),
+            pltpu.VMEM(x_codes.shape, jnp.int32),
+            pltpu.VMEM(y_codes.shape, jnp.int32),
             pltpu.VMEM((1, 2 * kpad), jnp.int32),
             pltpu.VMEM((chunks, 8, 2 * LANES), jnp.int32),
-            pltpu.VMEM((chunks, y_local, 2 * LANES), bf),
+            pltpu.VMEM((chunks - 1, y_local, 2 * LANES), bf),
             pltpu.VMEM((tall_y, 2 * LANES), f32),
             pltpu.VMEM((tall_y, 2 * LANES), f32),
             pltpu.VMEM((STEP, 2 * LANES), f32),
@@ -403,19 +532,58 @@
             pltpu.VMEM((chunks, modes, LANES), bf),
             pltpu.VMEM((chunks, modes, LANES), bf),
             pltpu.VMEM((chunks, modes, LANES), bf),
-            pltpu.VMEM((chunks, members, block, LANES), bf),
-            pltpu.VMEM((chunks, lead, block, 2 * LANES), bf),
+            pltpu.VMEM((chunks, lead, x_local, LANES), bf),
+            pltpu.VMEM((chunks - 1, lead, x_local, 2 * LANES), bf),
+            pltpu.VMEM((chunks, lead, kx, LANES), bf),
             dma, dma((chunks,)),
             dma, dma((chunks,)),
             dma, dma((chunks * pieces,)),
             dma, dma((chunks * lead,)),
             dma, dma((chunks * lead,)),
-            dma((2,)),
+            dma, dma((chunks * pieces,)),
+            dma, dma((chunks,)),
+            dma((3,)),
         ],
         compiler_params=pltpu.CompilerParams(
             collective_id=0, has_side_effects=True, vmem_limit_bytes=46 * 1024 * 1024
         ),
-    )(grid, codes)
+    )(*operands)
+
+
+def last_sum_kernel(order, spec_in, low_in, wide_in, y_in, spec_out, low_out, total, sem):
+    lead, x_local, _ = wide_in.shape
+    spot = lax.rem(lax.axis_index("gx"), lead)
+    spec_copy = pltpu.make_async_copy(spec_in, spec_out, sem.at[lead])
+
+    def field(source, t):
+        part = pl.ds(al(flipped(spot, t, lead) * x_local, x_local), x_local)
+        return pltpu.make_async_copy(source.at[part, :], low_out.at[part, :], sem.at[t])
+
+    field(low_in, 0).start()
+    spec_copy.start()
+    for t in order:
+        f = flipped(spot, t, lead)
+        part = pl.ds(al(f * x_local, x_local), x_local)
+        total[part, :] = low_in[part, :] + lax.dot_general(
+            wide_in[f], y_in[...], (((1,), (1,)), ((), ())), preferred_element_type=jnp.float32)
+        field(total, t).start()
+    field(low_in, 0).wait()
+    for t in order:
+        field(total, t).wait()
+    spec_copy.wait()
+
+
+def last_sum(spec, low, wide, y_table):
+    lead = wide.shape[0]
+    vmem, anywhere = pl.BlockSpec(memory_space=pltpu.VMEM), pl.BlockSpec(memory_space=pl.ANY)
+    return pl.pallas_call(
+        functools.partial(last_sum_kernel, near_first(lead)),
+        out_shape=(jax.ShapeDtypeStruct(spec.shape, spec.dtype), jax.ShapeDtypeStruct(low.shape, low.dtype)),
+        in_specs=[vmem] * 4,
+        out_specs=(anywhere, anywhere),
+        scratch_shapes=[pltpu.VMEM(low.shape, low.dtype), pltpu.SemaphoreType.DMA((lead + 1,))],
+        compiler_params=pltpu.CompilerParams(vmem_limit_bytes=12 * 1024 * 1024),
+    )(spec, low, wide, y_table)
 
 
 def build(gx, gy):
@@ -432,12 +600,12 @@
         me_y = lax.axis_index("gy")
         y_first = me_y * y_local
         grid = fields.reshape(lead * x_local, y_local)
-        fits = gy == 2 and gx == 4 * lead and kpad % LANES == 0 and kpad >= 4 * LANES and kx % 16 == 0
+        fits = gy == 2 and gx == 4 * lead and lead & (lead - 1) == 0 and kpad == 4 * LANES and kx % 16 == 0
         fits = fits and x_local % 16 == 0 and 2 * lead * x_local % (8 * STEP) == 0
         fits = fits and y_local % (8 * STEP) == 0 and gx * kx % (4 * LANES) == 0
         if fits:
-            spec, low = spectral_filter(
-                lead, x_local, kx, ky, kpad, grid, jnp.concatenate([x_codes, y_codes]).reshape(1, -1))
+            spec, low = last_sum(*spectral_filter(
+                lead, x_local, kx, ky, kpad, grid, x_codes.reshape(1, -1), y_codes.reshape(1, -1)))
             return spec.reshape(nf, nz, kx, ky), low.reshape(nf, nz, x_local, y_local)
         padded = jnp.pad(y_codes.reshape(gy, ky), ((0, 0), (0, kpad - ky)))
         live = jnp.broadcast_to(jnp.arange(kpad)[None] < ky, (gy, kpad)).reshape(-1)

time: 57.8 us -> 53.5 us (0.926)
  local copies, waits for them, and re-layouts: 4.65 us -> 0 us
  Pallas kernels: 51.6 us -> 52.6 us
  other arithmetic: 0.71 us -> 0 us
    unnamed x4 -> x0, local copies, waits for them, and re-layouts: 4.65 us -> none
    pallas_call x0 -> x1, Pallas kernels: none -> 2.67 us  [last_sum(): pl.pallas_call(functools.partial(last_sum_kernel, near_first(lead)), out_...]
    pallas_call x1, Pallas kernels: 51.6 us -> 50 us  [spectral_filter(): pl.pallas_call(functools.partial(filter_kernel, lead, x_local, kx, ky, kp...]
    concatenate x1 -> x0, other arithmetic: 0.71 us -> none  [local(): jnp.concatenate([x_codes, y_codes]).reshape(1, -1)]
where the time goes in v2:
time: 53.5 us; the launch traced here: 53.3 us
  Pallas kernels  52.6 us (98%)
  between operations  0.64 us (1%)
    pallas_call x1, Pallas kernels, spectral_filter(): pl.pallas_call(functools.partial(filter_kernel, lead, x_local, kx, ky, kp...  50 us
    pallas_call x1, Pallas kernels, last_sum(): pl.pallas_call(functools.partial(last_sum_kernel, near_first(lead)), out_...  2.67 us

profile of v2, /device:TPU:0, one launch (start us, length us, event | category | flops | bytes accessed | tf_op | source)
XLA Modules:
  0.0 53.3 jit_solution(15858617434711612926)
XLA Ops:
  0.6 50.0 %shard_map.50 = (f32[256,510]{1,0:T(8,128)S(1)}, f32[768,1536]{1,0:T(8,128)S(1)}, bf16[4,192,256]{2,1,0:T(8,128)(2,1)S(1)}, bf16[1536,256]{1,0:T(8,128)(2,1)S(1)}) custom-call(bf16[768,1536]{1,0:T(8,128)(2,1)} %bitcast.9, s32[1,1024]{1,0:T(1,128)} %bitcast.10, s32[1,1020]{1,0:T(1,128)} %bitcast.11), custom_call_target="tpu_custom_call" | custom-call | tf_op jit(solution)/shard_map/pallas_call | solution.py:499
  50.6 2.7 %shard_map.51 = (f32[256,510]{1,0:T(8,128)}, f32[768,1536]{1,0:T(8,128)}) custom-call(f32[256,510]{1,0:T(8,128)S(1)} %get-tuple-element.8.spec_in, f32[768,1536]{1,0:T(8,128)S(1)} %get-tuple-element.9.low_in, bf16[4,192,256]{2,1,0:T(8,128)(2,1)S(1)} %get-tuple-element.10.wide_in, bf16[1536,256]{1,0:T(8,128)(2,1)S(1)} %get-tuple-element.11.y_in), custom_call_target="tpu_custom_call" | custom-call | tf_op jit(solution)/shard_map/pallas_call | solution.py:579

commit v3 on v2

--- a/solution.py
+++ b/solution.py
@@ -131,11 +131,15 @@
     is_hub = plane == 1 + side
     across = (2 - side) * lead + spot
 
-    grid_copy = pltpu.make_async_copy(grid_in, grid_ref, in_sem.at[0])
-    ycode_copy = pltpu.make_async_copy(ycode_in, ycode_ref, in_sem.at[1])
-    xcode_copy = pltpu.make_async_copy(xcode_in, xcode_ref, in_sem.at[2])
+    def grid_copy(f):
+        part = pl.ds(al(f * x_local, x_local), x_local)
+        return pltpu.make_async_copy(grid_in.at[part, :], grid_ref.at[part, :], in_sem.at[2 + f])
+
+    ycode_copy = pltpu.make_async_copy(ycode_in, ycode_ref, in_sem.at[0])
+    xcode_copy = pltpu.make_async_copy(xcode_in, xcode_ref, in_sem.at[1])
     ycode_copy.start()
-    grid_copy.start()
+    for f in range(lead):
+        grid_copy(f).start()
     xcode_copy.start()
     barrier = pltpu.get_barrier_semaphore()
     pl.semaphore_signal(barrier, inc=1, device_id={"gy": peer})
@@ -152,6 +156,10 @@
         return flipped(spot, t, lead)
 
     far_first = near_first(lead)[::-1]
+    last = chunks - 1
+
+    def slot(k, i):
+        return k if k < last else last + i
 
     def wide_at(k):
         return wide_last if k == chunks - 1 else wide.at[k]
@@ -188,13 +196,13 @@
     def relay(k, m):
         view = coarse.at[k, span(m, piece), :]
         return pltpu.make_async_remote_copy(
-            src_ref=view, dst_ref=view, send_sem=s5, recv_sem=r5.at[k * pieces + m],
+            src_ref=view, dst_ref=view, send_sem=s5, recv_sem=r5.at[slot(k, m)],
             device_id={"gx": end_base + spot})
 
     def down(k, f):
         return pltpu.make_async_remote_copy(
             src_ref=blocks.at[k, f], dst_ref=wide_at(k).at[spot, :, span(half, LANES)],
-            send_sem=s3, recv_sem=r3.at[k * lead + spot], device_id={"gx": own_base + f})
+            send_sem=s3, recv_sem=r3.at[slot(k, spot)], device_id={"gx": own_base + f})
 
     def show(k, f):
         return pltpu.make_async_remote_copy(
@@ -209,12 +217,27 @@
     def down_in(k, f):
         return pltpu.make_async_remote_copy(
             src_ref=blocks.at[k, 0], dst_ref=wide_at(k).at[f, :, span(half, LANES)],
-            send_sem=s3, recv_sem=r3.at[k * lead + f], device_id={"gx": own_base + f})
+            send_sem=s3, recv_sem=r3.at[slot(k, f)], device_id={"gx": own_base + f})
+
+    def all_down(k):
+        view = wide.at[k, pl.ds(0, lead - 1), :, span(half, LANES)]
+        return pltpu.make_async_remote_copy(
+            src_ref=view, dst_ref=view, send_sem=s3, recv_sem=r3.at[k], device_id={"gx": own_base})
+
+    def all_forward(k, who):
+        place = wide.at[k, :, :, span(who, LANES)]
+        return pltpu.make_async_remote_copy(
+            src_ref=place, dst_ref=place, send_sem=s4, recv_sem=r4.at[k], device_id={"gy": peer})
+
+    def all_relayed(k):
+        view = coarse.at[k]
+        return pltpu.make_async_remote_copy(
+            src_ref=view, dst_ref=view, send_sem=s5, recv_sem=r5.at[k], device_id={"gx": hub_base})
 
     def forward(k, f, who):
         place = wide_at(k).at[f, :, span(who, LANES)]
         return pltpu.make_async_remote_copy(
-            src_ref=place, dst_ref=place, send_sem=s4, recv_sem=r4.at[k * lead + f],
+            src_ref=place, dst_ref=place, send_sem=s4, recv_sem=r4.at[slot(k, f)],
             device_id={"gy": peer})
 
     def local(f):
@@ -238,15 +261,23 @@
         with scope("ytab"):
             make_table(y_codes[k, :1, :], half * grid_ref.shape[1], NY, y_at(k), yta, ytb, yfc, yfs)
 
+    def field_sums(k, part):
+        both = jnp.dot(grid_ref[part, :], y_at(k)[...], preferred_element_type=f32)
+        low_part, high_part = both[:, :LANES], both[:, LANES:]
+        other[k, part, :] = jnp.where(half == 0, high_part, low_part).astype(bf)
+        own[k, part, :] = jnp.where(half == 0, low_part, high_part)
+
     def sums(k):
         if k == 0:
-            with scope("gridwait"):
-                grid_copy.wait()
-        with scope("dotA"):
-            both = jnp.dot(grid_ref[...], y_at(k)[...], preferred_element_type=f32)
-            low_part, high_part = both[:, :LANES], both[:, LANES:]
-            other[k] = jnp.where(half == 0, high_part, low_part).astype(bf)
-            own[k] = jnp.where(half == 0, low_part, high_part)
+            @pl.loop(0, lead)
+            def _(f):
+                with scope("gridwait"):
+                    grid_copy(f).wait()
+                with scope("dotA"):
+                    field_sums(k, span(f, x_local))
+        else:
+            with scope("dotA"):
+                field_sums(k, pl.ds(0, rows))
         if k == 0:
             with scope("barrier"):
                 pl.semaphore_wait(barrier, members + jnp.where(is_hub, 1, 0))
@@ -268,22 +299,22 @@
         def _():
             lines[k, span(mine, x_local), :] = part[k, span(spot, x_local), :]
 
-    def partial_sum(k, held=1):
+    def gather(k):
         with scope("upwait"):
             up_in(k).wait_recv()
 
         with scope("dotB"):
             turned[...] = lines[k].T
 
-            @pl.loop(0, pieces)
-            def _(m):
-                got = jnp.dot(turned[...], xt[:, span(m, piece)], preferred_element_type=f32).T
-                s_own[k, span(m, piece), :] = got
-                s_out[k, span(m, piece), :] = got.astype(bf)
-
-                @pl.when(half <= held)
-                def _():
-                    cross(k, m).start()
+    def partial_sum(k, m, held=1):
+        with scope("dotB"):
+            got = jnp.dot(turned[...], xt[:, pl.ds(m * piece, piece)], preferred_element_type=f32).T
+            s_own[k, pl.ds(m * piece, piece), :] = got
+            s_out[k, pl.ds(m * piece, piece), :] = got.astype(bf)
+
+        @pl.when(half <= held)
+        def _():
+            cross(k, m).start()
 
     mine_x = span(plane - 2 * side, rows)
 
@@ -313,10 +344,15 @@
         relay(k, m).start()
         absorb(k, m)
 
-    def receive(k, m):
-        with scope("relaywait"):
-            relay(k, m).wait_recv()
-        absorb(k, m)
+    def receive(k):
+        if k < last:
+            with scope("relaywait"):
+                all_relayed(k).wait_recv()
+        for m in range(pieces):
+            if k == last:
+                with scope("relaywait"):
+                    relay(k, m).wait_recv()
+            absorb(k, m)
 
     def synthesis(k):
         if k < chunks - 1:
@@ -335,14 +371,6 @@
         def _():
             share(k)
 
-    def pass_on(k, f):
-        @pl.when(f != spot)
-        def _():
-            with scope("downwait"):
-                down_in(k, f).wait_recv()
-
-        forward(k, f, half).start()
-
     def reveal(k):
         with scope("showwait"):
             show_in(k).wait_recv()
@@ -351,8 +379,6 @@
             found[k].reshape(lead * kx, LANES)[:, :columns].astype(f32))
 
     def add_field(k, f):
-        with scope("fwdwait"):
-            forward(k, f, peer).wait_recv()
         with scope("dotD"):
             got = lax.dot_general(
                 wide_at(k)[f], y_at(k)[...], (((1,), (1,)), ((), ())), preferred_element_type=f32)
@@ -360,30 +386,32 @@
                 got = got + low_ref[span(f, x_local), :]
             low_ref[span(f, x_local), :] = got
 
-    def turn_of(t):
-        return lax.rem(spot + lead - lax.rem(t, lead), lead)
-
     def take(k):
-        @pl.loop(1, lead + 1)
-        def _(t):
-            pass_on(k, turn_of(t))
-
+        with scope("downwait"):
+            all_down(k).wait_recv()
+        all_forward(k, half).start()
         reveal(k)
 
     def expand(k):
-        @pl.loop(1, lead + 1)
-        def _(t):
-            add_field(k, turn_of(t))
+        with scope("fwdwait"):
+            all_forward(k, peer).wait_recv()
+
+        @pl.loop(0, lead)
+        def _(f):
+            add_field(k, f)
 
     def finish():
-        k = chunks - 1
-        add_field(k, spot)
+        with scope("fwdwait"):
+            forward(last, spot, peer).wait_recv()
+        add_field(last, spot)
         for t in reversed(far_first):
-            pass_on(k, mate(t))
-        reveal(k)
+            with scope("downwait"):
+                down_in(last, mate(t)).wait_recv()
+            forward(last, mate(t), half).start()
+        reveal(last)
         with scope("fwdwait"):
             for t in reversed(far_first):
-                forward(k, mate(t), peer).wait_recv()
+                forward(last, mate(t), peer).wait_recv()
 
     y_table(0)
     sums(0)
@@ -395,6 +423,7 @@
 
     sums(1)
     y_table(2)
+    y_table(3)
 
     @pl.when(half == 1)
     def _():
@@ -410,13 +439,14 @@
         x_table()
         rise(1)
         sums(2)
-        y_table(3)
 
         @pl.when(half == 1)
         def _():
             sums(3)
 
-        partial_sum(0)
+        gather(0)
+        for m in range(pieces):
+            partial_sum(0, m)
 
         @pl.when(half == 0)
         def _():
@@ -424,16 +454,20 @@
 
         rise(2)
         rise(3)
-        partial_sum(1)
         for k in range(chunks):
-            ahead = pieces - 1 - k
-            for m in range(ahead):
+            more = k + 1 < chunks
+            held = 0 if k + 2 == chunks else 1
+            meet(k, 0)
+            if more:
+                gather(k + 1)
+                for m in range(pieces // 2):
+                    partial_sum(k + 1, m, held)
+            meet(k, 1)
+            if more:
+                for m in range(pieces // 2, pieces):
+                    partial_sum(k + 1, m, held)
+            for m in range(2, pieces):
                 meet(k, m)
-            if k + 2 < chunks:
-                partial_sum(k + 2, 0 if k + 3 == chunks else 1)
-            for m in range(ahead, pieces):
-                meet(k, m)
-            synthesis(k)
             if k == chunks - 2:
                 @pl.when(half == 1)
                 def _():
@@ -441,31 +475,62 @@
                     def _(m):
                         cross(chunks - 1, m).start()
 
+            synthesis(k)
+            if k == chunks - 2:
+                for early in range(chunks - 2):
+                    take(early)
+
+                @pl.when(half == 1)
+                def _():
+                    expand(0)
+
         forward(chunks - 1, spot, half).start()
-        for k in range(chunks - 1):
-            take(k)
-            expand(k)
+
+        @pl.when(half == 0)
+        def _():
+            for k in range(chunks - 2):
+                expand(k)
+
+        take(chunks - 2)
+
+        @pl.when(half == 1)
+        def _():
+            for k in range(1, chunks - 2):
+                expand(k)
+
+        expand(chunks - 2)
         finish()
 
     @pl.when(jnp.logical_not(is_hub))
     def _():
         sums(2)
-        y_table(3)
-
+        sums(3)
         rise(1)
-        sums(3)
         rise(2)
         rise(3)
         x_table()
-        for k in range(chunks):
-            for m in range(pieces):
-                receive(k, m)
+        for k in range(last):
+            receive(k)
             synthesis(k)
-            if k == chunks - 1:
-                forward(k, spot, half).start()
             if k > 0:
                 take(k - 1)
-                expand(k - 1)
+                if k < last - 1:
+                    expand(k - 1)
+
+        @pl.when(half == 1)
+        def _():
+            expand(last - 2)
+
+        receive(last)
+        synthesis(last)
+        forward(last, spot, half).start()
+
+        @pl.when(half == 0)
+        def _():
+            expand(last - 2)
+
+        take(last - 1)
+        expand(last - 1)
         finish()
 
     with scope("drain"):
@@ -538,11 +603,11 @@
             dma, dma((chunks,)),
             dma, dma((chunks,)),
             dma, dma((chunks * pieces,)),
-            dma, dma((chunks * lead,)),
-            dma, dma((chunks * lead,)),
-            dma, dma((chunks * pieces,)),
+            dma, dma((chunks - 1 + lead,)),
+            dma, dma((chunks - 1 + lead,)),
+            dma, dma((chunks - 1 + pieces,)),
             dma, dma((chunks,)),
-            dma((3,)),
+            dma((2 + lead,)),
         ],
         compiler_params=pltpu.CompilerParams(
             collective_id=0, has_side_effects=True, vmem_limit_bytes=46 * 1024 * 1024

time: 53.5 us -> 52 us (0.972)
  Pallas kernels: 52.6 us -> 51 us
    pallas_call x1, Pallas kernels: 50 us -> 48.3 us  [spectral_filter(): pl.pallas_call(functools.partial(filter_kernel, lead, x_local, kx, ky, kp...]
where the time goes in v3:
time: 52 us; the launch traced here: 51.8 us
  Pallas kernels  51 us (98%)
  between operations  0.82 us (2%)
    pallas_call x1, Pallas kernels, spectral_filter(): pl.pallas_call(functools.partial(filter_kernel, lead, x_local, kx, ky, kp...  48.3 us
    pallas_call x1, Pallas kernels, last_sum(): pl.pallas_call(functools.partial(last_sum_kernel, near_first(lead)), out_...  2.67 us

profile of v3, /device:TPU:0, one launch (start us, length us, event | category | flops | bytes accessed | tf_op | source)
XLA Modules:
  0.0 51.8 jit_solution(9171546396291037372)
XLA Ops:
  0.6 48.3 %shard_map.50 = (f32[256,510]{1,0:T(8,128)S(1)}, f32[768,1536]{1,0:T(8,128)S(1)}, bf16[4,192,256]{2,1,0:T(8,128)(2,1)S(1)}, bf16[1536,256]{1,0:T(8,128)(2,1)S(1)}) custom-call(bf16[768,1536]{1,0:T(8,128)(2,1)} %bitcast.9, s32[1,1024]{1,0:T(1,128)} %bitcast.10, s32[1,1020]{1,0:T(1,128)} %bitcast.11), custom_call_target="tpu_custom_call" | custom-call | tf_op jit(solution)/shard_map/pallas_call | solution.py:564
  48.9 2.7 %shard_map.51 = (f32[256,510]{1,0:T(8,128)}, f32[768,1536]{1,0:T(8,128)}) custom-call(f32[256,510]{1,0:T(8,128)S(1)} %get-tuple-element.8.spec_in, f32[768,1536]{1,0:T(8,128)S(1)} %get-tuple-element.9.low_in, bf16[4,192,256]{2,1,0:T(8,128)(2,1)S(1)} %get-tuple-element.10.wide_in, bf16[1536,256]{1,0:T(8,128)(2,1)S(1)} %get-tuple-element.11.y_in), custom_call_target="tpu_custom_call" | custom-call | tf_op jit(solution)/shard_map/pallas_call | solution.py:644

commit v4 on v3

--- a/solution.py
+++ b/solution.py
@@ -107,8 +107,8 @@
     lead, x_local, kx, ky, kpad,
     grid_in, xcode_in, ycode_in, spec_ref, low_ref, wide_last, y_last,
     grid_ref, xcode_ref, ycode_ref, y_raw, y_codes, y_ref, yta, ytb, yfc, yfs, own, other, inc, part, lines, turned, xt, xta, xtb, xfc, xfs,
-    s_own, s_out, s_in, coarse, blocks, wide, found,
-    gs, gr, s1, r1, s2, r2, s3, r3, s4, r4, s5, r5, s6, r6, in_sem,
+    s_own, s_out, s_in, coarse, blocks, wide, found, far,
+    gs, gr, s1, r1, s2, r2, s3, r3, s4, r4, s5, r5, s6, r6, s7, in_sem,
 ):
     me = lax.axis_index("gx")
     half = lax.axis_index("gy")
@@ -323,6 +323,42 @@
             show(k, mate(t)).start()
         found[k, spot] = coarse[k, span(me, kx), :]
 
+    far_plane = 3 * side
+    far_x = span(far_plane - 2 * side, rows)
+
+    def throw(f):
+        return pltpu.make_async_remote_copy(
+            src_ref=far.at[f], dst_ref=wide_last.at[spot, :, span(half, LANES)],
+            send_sem=s7.at[0], recv_sem=r3.at[slot(last, spot)], device_id={"gx": far_plane * lead + f})
+
+    def throw_modes():
+        for t in far_first + [0]:
+            f = mate(t)
+            pltpu.make_async_remote_copy(
+                src_ref=coarse.at[last, span(far_plane * lead + f, kx), :], dst_ref=found.at[last, spot],
+                send_sem=s7.at[1], recv_sem=r6.at[last], device_id={"gx": far_plane * lead + f}).start()
+
+    def absorb_far(m):
+        if m < pieces - 1:
+            @pl.when(far_plane == m)
+            def _():
+                throw_modes()
+
+        with scope("dotF"):
+            got = jnp.dot(
+                xt[far_x, pl.ds(m * piece, piece)], coarse[last, pl.ds(m * piece, piece), :],
+                preferred_element_type=f32)
+            if m < pieces - 1:
+                own[1] = got if m == 0 else own[1] + got
+            else:
+                far[...] = (own[1] + got).astype(bf).reshape(lead, x_local, LANES)
+                for t in far_first + [0]:
+                    throw(mate(t)).start()
+
+                @pl.when(far_plane == m)
+                def _():
+                    throw_modes()
+
     def absorb(k, m):
         if m < pieces - 1:
             @pl.when(plane == m)
@@ -341,7 +377,17 @@
             cross(k, m).wait_recv()
         part_of = pl.ds(m * piece, piece)
         coarse[k, part_of, :] = (s_own[k, part_of, :] + s_in[k, part_of, :].astype(f32)).astype(bf)
-        relay(k, m).start()
+        if k < last:
+            relay(k, m).start()
+        else:
+            @pl.when(half == 0)
+            def _():
+                relay(k, m).start()
+
+            @pl.when(half == 1)
+            def _():
+                absorb_far(m)
+
         absorb(k, m)
 
     def receive(k):
@@ -374,6 +420,9 @@
     def reveal(k):
         with scope("showwait"):
             show_in(k).wait_recv()
+        write_modes(k)
+
+    def write_modes(k):
         columns = min(LANES, ky - k * LANES)
         spec_ref[:, pl.ds(k * LANES, columns)] = (
             found[k].reshape(lead * kx, LANES)[:, :columns].astype(f32))
@@ -400,18 +449,36 @@
         def _(f):
             add_field(k, f)
 
-    def finish():
+    def own_first():
         with scope("fwdwait"):
             forward(last, spot, peer).wait_recv()
         add_field(last, spot)
-        for t in reversed(far_first):
-            with scope("downwait"):
-                down_in(last, mate(t)).wait_recv()
-            forward(last, mate(t), half).start()
-        reveal(last)
+
+    def pass_on(t):
+        with scope("downwait"):
+            down_in(last, mate(t)).wait_recv()
+        forward(last, mate(t), half).start()
+
+    def others():
         with scope("fwdwait"):
             for t in reversed(far_first):
                 forward(last, mate(t), peer).wait_recv()
+
+    def finish():
+        @pl.when(half == 0)
+        def _():
+            for t in reversed(far_first):
+                pass_on(t)
+            own_first()
+
+        @pl.when(half == 1)
+        def _():
+            own_first()
+            for t in reversed(far_first):
+                pass_on(t)
+
+        reveal(last)
+        others()
 
     y_table(0)
     sums(0)
@@ -521,34 +588,73 @@
         def _():
             expand(last - 2)
 
-        receive(last)
-        synthesis(last)
-        forward(last, spot, half).start()
-
         @pl.when(half == 0)
         def _():
+            receive(last)
+            synthesis(last)
+            forward(last, spot, half).start()
             expand(last - 2)
 
         take(last - 1)
         expand(last - 1)
-        finish()
+
+        @pl.when(half == 0)
+        def _():
+            for t in reversed(far_first):
+                pass_on(t)
+            own_first()
+            reveal(last)
+
+        @pl.when(half == 1)
+        def _():
+            pass_on(0)
+            own_first()
+            for t in reversed(far_first):
+                pass_on(t)
+            all_found = found.at[last]
+            with scope("showwait"):
+                pltpu.make_async_remote_copy(
+                    src_ref=all_found, dst_ref=all_found, send_sem=s6, recv_sem=r6.at[last],
+                    device_id={"gx": own_base}).wait_recv()
+            write_modes(last)
+
+        others()
 
     with scope("drain"):
         sent(other, gs)
         sent(wide.at[:, :, :, pl.ds(0, LANES)], s4)
         sent(wide_last.at[:, :, pl.ds(0, LANES)], s4)
-        sent(found.at[:, pl.ds(0, lead - 1)], s6)
-        sent(blocks.at[:, pl.ds(0, lead - 1)], s3)
 
         @pl.when(is_hub)
         def _():
             sent(part.at[:, pl.ds(0, rows - x_local), :], s1)
             sent(s_out, s2)
-            sent(coarse, s5)
+            sent(found.at[:, pl.ds(0, lead - 1)], s6)
+            sent(blocks.at[:, pl.ds(0, lead - 1)], s3)
+
+            @pl.when(half == 0)
+            def _():
+                sent(coarse, s5)
+
+            @pl.when(half == 1)
+            def _():
+                sent(coarse.at[pl.ds(0, last)], s5)
+                sent(far, s7.at[0])
+                sent(found.at[last], s7.at[1])
 
         @pl.when(jnp.logical_not(is_hub))
         def _():
             sent(part, s1)
+
+            @pl.when(half == 0)
+            def _():
+                sent(found.at[:, pl.ds(0, lead - 1)], s6)
+                sent(blocks.at[:, pl.ds(0, lead - 1)], s3)
+
+            @pl.when(half == 1)
+            def _():
+                sent(found.at[pl.ds(0, last), pl.ds(0, lead - 1)], s6)
+                sent(blocks.at[pl.ds(0, last), pl.ds(0, lead - 1)], s3)
 
 
 def spectral_filter(lead, x_local, kx, ky, kpad, *operands):
@@ -600,6 +706,7 @@
             pltpu.VMEM((chunks, lead, x_local, LANES), bf),
             pltpu.VMEM((chunks - 1, lead, x_local, 2 * LANES), bf),
             pltpu.VMEM((chunks, lead, kx, LANES), bf),
+            pltpu.VMEM((lead, x_local, LANES), bf),
             dma, dma((chunks,)),
             dma, dma((chunks,)),
             dma, dma((chunks * pieces,)),
@@ -607,6 +714,7 @@
             dma, dma((chunks - 1 + lead,)),
             dma, dma((chunks - 1 + pieces,)),
             dma, dma((chunks,)),
+            dma((2,)),
             dma((2 + lead,)),
         ],
         compiler_params=pltpu.CompilerParams(

time: 52 us -> 50.8 us (0.977)
  Pallas kernels: 51 us -> 49.9 us
    pallas_call x1, Pallas kernels: 48.3 us -> 47.2 us  [spectral_filter(): pl.pallas_call(functools.partial(filter_kernel, lead, x_local, kx, ky, kp...]
where the time goes in v4:
time: 50.8 us; the launch traced here: 50.7 us
  Pallas kernels  49.9 us (98%)
  between operations  0.8 us (2%)
    pallas_call x1, Pallas kernels, spectral_filter(): pl.pallas_call(functools.partial(filter_kernel, lead, x_local, kx, ky, kp...  47.2 us
    pallas_call x1, Pallas kernels, last_sum(): pl.pallas_call(functools.partial(last_sum_kernel, near_first(lead)), out_...  2.67 us

profile of v4, /device:TPU:0, one launch (start us, length us, event | category | flops | bytes accessed | tf_op | source)
XLA Modules:
  0.0 50.7 jit_solution(17403793512383532861)
XLA Ops:
  0.6 47.2 %shard_map.50 = (f32[256,510]{1,0:T(8,128)S(1)}, f32[768,1536]{1,0:T(8,128)S(1)}, bf16[4,192,256]{2,1,0:T(8,128)(2,1)S(1)}, bf16[1536,256]{1,0:T(8,128)(2,1)S(1)}) custom-call(bf16[768,1536]{1,0:T(8,128)(2,1)} %bitcast.9, s32[1,1024]{1,0:T(1,128)} %bitcast.10, s32[1,1020]{1,0:T(1,128)} %bitcast.11), custom_call_target="tpu_custom_call" | custom-call | tf_op jit(solution)/shard_map/pallas_call | solution.py:670
  47.8 2.7 %shard_map.51 = (f32[256,510]{1,0:T(8,128)}, f32[768,1536]{1,0:T(8,128)}) custom-call(f32[256,510]{1,0:T(8,128)S(1)} %get-tuple-element.8.spec_in, f32[768,1536]{1,0:T(8,128)S(1)} %get-tuple-element.9.low_in, bf16[4,192,256]{2,1,0:T(8,128)(2,1)S(1)} %get-tuple-element.10.wide_in, bf16[1536,256]{1,0:T(8,128)(2,1)S(1)} %get-tuple-element.11.y_in), custom_call_target="tpu_custom_call" | custom-call | tf_op jit(solution)/shard_map/pallas_call | solution.py:752

commit v5 on v4

--- a/solution.py
+++ b/solution.py
@@ -63,8 +63,8 @@
 LANES = 128
 
 
-def make_table(code, first, length, table, ta, tb, fc, fs):
-    amount, codes = table.shape
+def make_table(code, first, length, table, side, ta, tb, fc, fs):
+    amount, codes = table.shape[0], code.shape[1]
     f32 = jnp.float32
     freq = jnp.where(code <= BAND, code, code - BAND).astype(f32)
     shift = jnp.where(code <= BAND, 0, 1).astype(f32)
@@ -86,7 +86,7 @@
 
     @pl.loop(0, amount // STEP)
     def _(h):
-        table[pl.ds(al(h * STEP, STEP), STEP), :] = (
+        table[pl.ds(al(h * STEP, STEP), STEP), side] = (
             ta[pl.ds(h, 1), :] * fc[...] - tb[pl.ds(h, 1), :] * fs[...]
         ).astype(jnp.bfloat16)
 
@@ -161,11 +161,27 @@
     def slot(k, i):
         return k if k < last else last + i
 
-    def wide_at(k):
-        return wide_last if k == chunks - 1 else wide.at[k]
+    def late(k):
+        return pl.ds((k - chunks + 2) * 2 * LANES, 2 * LANES)
+
+    def wide_at(k, who):
+        if k >= chunks - 2:
+            return wide_last, pl.ds(al((2 * (k - chunks + 2) + who) * LANES, LANES), LANES)
+        return wide.at[k], span(who, LANES)
+
+    def wide_row(k, f, who):
+        ref, columns = wide_at(k, who)
+        return ref.at[f, :, columns]
+
+    def both_halves(k, f):
+        return wide_last[f, :, late(k)] if k >= chunks - 2 else wide[k, f]
+
+    def y_place(k):
+        return (y_last, late(k)) if k >= chunks - 2 else (y_ref.at[k], slice(None))
 
     def y_at(k):
-        return y_last if k == chunks - 1 else y_ref.at[k]
+        ref, columns = y_place(k)
+        return ref[:, columns]
 
     def span(i, n):
         return pl.ds(al(i * n, n), n)
@@ -201,7 +217,7 @@
 
     def down(k, f):
         return pltpu.make_async_remote_copy(
-            src_ref=blocks.at[k, f], dst_ref=wide_at(k).at[spot, :, span(half, LANES)],
+            src_ref=blocks.at[k, f], dst_ref=wide_row(k, spot, half),
             send_sem=s3, recv_sem=r3.at[slot(k, spot)], device_id={"gx": own_base + f})
 
     def show(k, f):
@@ -216,16 +232,18 @@
 
     def down_in(k, f):
         return pltpu.make_async_remote_copy(
-            src_ref=blocks.at[k, 0], dst_ref=wide_at(k).at[f, :, span(half, LANES)],
+            src_ref=blocks.at[k, 0], dst_ref=wide_row(k, f, half),
             send_sem=s3, recv_sem=r3.at[slot(k, f)], device_id={"gx": own_base + f})
 
     def all_down(k):
-        view = wide.at[k, pl.ds(0, lead - 1), :, span(half, LANES)]
+        ref, columns = wide_at(k, half)
+        view = ref.at[pl.ds(0, lead - 1), :, columns]
         return pltpu.make_async_remote_copy(
             src_ref=view, dst_ref=view, send_sem=s3, recv_sem=r3.at[k], device_id={"gx": own_base})
 
     def all_forward(k, who):
-        place = wide.at[k, :, :, span(who, LANES)]
+        ref, columns = wide_at(k, who)
+        place = ref.at[:, :, columns]
         return pltpu.make_async_remote_copy(
             src_ref=place, dst_ref=place, send_sem=s4, recv_sem=r4.at[k], device_id={"gy": peer})
 
@@ -235,7 +253,7 @@
             src_ref=view, dst_ref=view, send_sem=s5, recv_sem=r5.at[k], device_id={"gx": hub_base})
 
     def forward(k, f, who):
-        place = wide_at(k).at[f, :, span(who, LANES)]
+        place = wide_row(k, f, who)
         return pltpu.make_async_remote_copy(
             src_ref=place, dst_ref=place, send_sem=s4, recv_sem=r4.at[slot(k, f)],
             device_id={"gy": peer})
@@ -259,10 +277,10 @@
 
     def y_table(k):
         with scope("ytab"):
-            make_table(y_codes[k, :1, :], half * grid_ref.shape[1], NY, y_at(k), yta, ytb, yfc, yfs)
+            make_table(y_codes[k, :1, :], half * grid_ref.shape[1], NY, *y_place(k), yta, ytb, yfc, yfs)
 
     def field_sums(k, part):
-        both = jnp.dot(grid_ref[part, :], y_at(k)[...], preferred_element_type=f32)
+        both = jnp.dot(grid_ref[part, :], y_at(k), preferred_element_type=f32)
         low_part, high_part = both[:, :LANES], both[:, LANES:]
         other[k, part, :] = jnp.where(half == 0, high_part, low_part).astype(bf)
         own[k, part, :] = jnp.where(half == 0, low_part, high_part)
@@ -328,7 +346,7 @@
 
     def throw(f):
         return pltpu.make_async_remote_copy(
-            src_ref=far.at[f], dst_ref=wide_last.at[spot, :, span(half, LANES)],
+            src_ref=far.at[f], dst_ref=wide_row(last, spot, half),
             send_sem=s7.at[0], recv_sem=r3.at[slot(last, spot)], device_id={"gx": far_plane * lead + f})
 
     def throw_modes():
@@ -411,7 +429,8 @@
         for t in far_first:
             down(k, mate(t)).start()
 
-        wide_at(k)[spot, :, span(half, LANES)] = blocks[k, spot]
+        ref, columns = wide_at(k, half)
+        ref[spot, :, columns] = blocks[k, spot]
 
         @pl.when(plane == pieces - 1)
         def _():
@@ -430,7 +449,7 @@
     def add_field(k, f):
         with scope("dotD"):
             got = lax.dot_general(
-                wide_at(k)[f], y_at(k)[...], (((1,), (1,)), ((), ())), preferred_element_type=f32)
+                both_halves(k, f), y_at(k), (((1,), (1,)), ((), ())), preferred_element_type=f32)
             if k > 0:
                 got = got + low_ref[span(f, x_local), :]
             low_ref[span(f, x_local), :] = got
@@ -445,6 +464,10 @@
         with scope("fwdwait"):
             all_forward(k, peer).wait_recv()
 
+        if k == last - 1:
+            add_field(k, spot)
+            return
+
         @pl.loop(0, lead)
         def _(f):
             add_field(k, f)
@@ -499,7 +522,7 @@
     def x_table():
         with scope("xtab"):
             xcode_copy.wait()
-            make_table(xcode_ref[...], side * xt.shape[0], NX, xt, xta, xtb, xfc, xfs)
+            make_table(xcode_ref[...], side * xt.shape[0], NX, xt, slice(None), xta, xtb, xfc, xfs)
 
     @pl.when(is_hub)
     def _():
@@ -535,6 +558,7 @@
                     partial_sum(k + 1, m, held)
             for m in range(2, pieces):
                 meet(k, m)
+            synthesis(k)
             if k == chunks - 2:
                 @pl.when(half == 1)
                 def _():
@@ -542,7 +566,6 @@
                     def _(m):
                         cross(chunks - 1, m).start()
 
-            synthesis(k)
             if k == chunks - 2:
                 for early in range(chunks - 2):
                     take(early)
@@ -590,16 +613,23 @@
 
         @pl.when(half == 0)
         def _():
-            receive(last)
+            for m in range(pieces):
+                with scope("relaywait"):
+                    relay(last, m).wait_recv()
+                absorb(last, m)
+                if m == 0:
+                    with scope("fwdwait"):
+                        all_forward(last - 2, peer).wait_recv()
+                if m < pieces - 1:
+                    for f in range(m * lead // (pieces - 1), (m + 1) * lead // (pieces - 1)):
+                        add_field(last - 2, f)
             synthesis(last)
             forward(last, spot, half).start()
-            expand(last - 2)
 
         take(last - 1)
-        expand(last - 1)
-
         @pl.when(half == 0)
         def _():
+            expand(last - 1)
             for t in reversed(far_first):
                 pass_on(t)
             own_first()
@@ -607,10 +637,10 @@
 
         @pl.when(half == 1)
         def _():
-            pass_on(0)
+            for t in [0] + far_first[::-1]:
+                pass_on(t)
+            expand(last - 1)
             own_first()
-            for t in reversed(far_first):
-                pass_on(t)
             all_found = found.at[last]
             with scope("showwait"):
                 pltpu.make_async_remote_copy(
@@ -623,7 +653,7 @@
     with scope("drain"):
         sent(other, gs)
         sent(wide.at[:, :, :, pl.ds(0, LANES)], s4)
-        sent(wide_last.at[:, :, pl.ds(0, LANES)], s4)
+        sent(wide_last.at[:, :, pl.ds(0, 2 * LANES)], s4)
 
         @pl.when(is_hub)
         def _():
@@ -672,8 +702,8 @@
         out_shape=(
             jax.ShapeDtypeStruct((lead * kx, ky), f32),
             jax.ShapeDtypeStruct((rows, y_local), f32),
-            jax.ShapeDtypeStruct((lead, x_local, 2 * LANES), bf),
-            jax.ShapeDtypeStruct((y_local, 2 * LANES), bf),
+            jax.ShapeDtypeStruct((lead, x_local, 4 * LANES), bf),
+            jax.ShapeDtypeStruct((y_local, 4 * LANES), bf),
         ),
         in_specs=[pl.BlockSpec(memory_space=pltpu.HBM)] * 3,
         out_specs=(vmem,) * 4,
@@ -683,7 +713,7 @@
             pltpu.VMEM(y_codes.shape, jnp.int32),
             pltpu.VMEM((1, 2 * kpad), jnp.int32),
             pltpu.VMEM((chunks, 8, 2 * LANES), jnp.int32),
-            pltpu.VMEM((chunks - 1, y_local, 2 * LANES), bf),
+            pltpu.VMEM((chunks - 2, y_local, 2 * LANES), bf),
             pltpu.VMEM((tall_y, 2 * LANES), f32),
             pltpu.VMEM((tall_y, 2 * LANES), f32),
             pltpu.VMEM((STEP, 2 * LANES), f32),
@@ -704,7 +734,7 @@
             pltpu.VMEM((chunks, modes, LANES), bf),
             pltpu.VMEM((chunks, modes, LANES), bf),
             pltpu.VMEM((chunks, lead, x_local, LANES), bf),
-            pltpu.VMEM((chunks - 1, lead, x_local, 2 * LANES), bf),
+            pltpu.VMEM((chunks - 2, lead, x_local, 2 * LANES), bf),
             pltpu.VMEM((chunks, lead, kx, LANES), bf),
             pltpu.VMEM((lead, x_local, LANES), bf),
             dma, dma((chunks,)),
@@ -718,7 +748,7 @@
             dma((2 + lead,)),
         ],
         compiler_params=pltpu.CompilerParams(
-            collective_id=0, has_side_effects=True, vmem_limit_bytes=46 * 1024 * 1024
+            collective_id=0, has_side_effects=True, vmem_limit_bytes=44 * 1024 * 1024
         ),
     )(*operands)
 

time: 50.8 us -> 49.8 us (0.980)
  Pallas kernels: 49.9 us -> 48.8 us
    pallas_call x1, Pallas kernels: 47.2 us -> 46.1 us  [spectral_filter(): pl.pallas_call(functools.partial(filter_kernel, lead, x_local, kx, ky, kp...]
where the time goes in v5:
time: 49.8 us; the launch traced here: 49.6 us
  Pallas kernels  48.8 us (98%)
  between operations  0.8 us (2%)
    pallas_call x1, Pallas kernels, spectral_filter(): pl.pallas_call(functools.partial(filter_kernel, lead, x_local, kx, ky, kp...  46.1 us
    pallas_call x1, Pallas kernels, last_sum(): pl.pallas_call(functools.partial(last_sum_kernel, near_first(lead)), out_...  2.74 us

profile of v5, /device:TPU:0, one launch (start us, length us, event | category | flops | bytes accessed | tf_op | source)
XLA Modules:
  0.0 49.6 jit_solution(5459749239415741347)
XLA Ops:
  0.6 46.1 %shard_map.50 = (f32[256,510]{1,0:T(8,128)S(1)}, f32[768,1536]{1,0:T(8,128)S(1)}, bf16[4,192,512]{2,1,0:T(8,128)(2,1)S(1)}, bf16[1536,512]{1,0:T(8,128)(2,1)S(1)}) custom-call(bf16[768,1536]{1,0:T(8,128)(2,1)} %bitcast.9, s32[1,1024]{1,0:T(1,128)} %bitcast.10, s32[1,1020]{1,0:T(1,128)} %bitcast.11), custom_call_target="tpu_custom_call" | custom-call | tf_op jit(solution)/shard_map/pallas_call | solution.py:700
  46.7 2.7 %shard_map.51 = (f32[256,510]{1,0:T(8,128)}, f32[768,1536]{1,0:T(8,128)}) custom-call(f32[256,510]{1,0:T(8,128)S(1)} %get-tuple-element.8.spec_in, f32[768,1536]{1,0:T(8,128)S(1)} %get-tuple-element.9.low_in, bf16[4,192,512]{2,1,0:T(8,128)(2,1)S(1)} %get-tuple-element.10.wide_in, bf16[1536,512]{1,0:T(8,128)(2,1)S(1)} %get-tuple-element.11.y_in), custom_call_target="tpu_custom_call" | custom-call | tf_op jit(solution)/shard_map/pallas_call | solution.py:782

commit v6 on v5

--- a/solution.py
+++ b/solution.py
@@ -534,6 +534,7 @@
         def _():
             sums(3)
 
+        rise(2)
         gather(0)
         for m in range(pieces):
             partial_sum(0, m)
@@ -542,17 +543,26 @@
         def _():
             sums(3)
 
-        rise(2)
         rise(3)
         for k in range(chunks):
             more = k + 1 < chunks
             held = 0 if k + 2 == chunks else 1
             meet(k, 0)
+            if k == 0:
+                @pl.when(half == 0)
+                def _():
+                    meet(0, 1)
+
             if more:
                 gather(k + 1)
                 for m in range(pieces // 2):
                     partial_sum(k + 1, m, held)
-            meet(k, 1)
+            if k == 0:
+                @pl.when(half == 1)
+                def _():
+                    meet(0, 1)
+            else:
+                meet(k, 1)
             if more:
                 for m in range(pieces // 2, pieces):
                     partial_sum(k + 1, m, held)

time: 49.8 us -> 49.8 us (level)
  no operation moved by 1% of the time
where the time goes in v6:
time: 49.8 us; the launch traced here: 49.6 us
  Pallas kernels  48.8 us (98%)
  between operations  0.8 us (2%)
    pallas_call x1, Pallas kernels, spectral_filter(): pl.pallas_call(functools.partial(filter_kernel, lead, x_local, kx, ky, kp...  46.1 us
    pallas_call x1, Pallas kernels, last_sum(): pl.pallas_call(functools.partial(last_sum_kernel, near_first(lead)), out_...  2.74 us

profile of v6, /device:TPU:0, one launch (start us, length us, event | category | flops | bytes accessed | tf_op | source)
XLA Modules:
  0.0 49.6 jit_solution(2164241138757857131)
XLA Ops:
  0.6 46.1 %shard_map.50 = (f32[256,510]{1,0:T(8,128)S(1)}, f32[768,1536]{1,0:T(8,128)S(1)}, bf16[4,192,512]{2,1,0:T(8,128)(2,1)S(1)}, bf16[1536,512]{1,0:T(8,128)(2,1)S(1)}) custom-call(bf16[768,1536]{1,0:T(8,128)(2,1)} %bitcast.9, s32[1,1024]{1,0:T(1,128)} %bitcast.10, s32[1,1020]{1,0:T(1,128)} %bitcast.11), custom_call_target="tpu_custom_call" | custom-call | tf_op jit(solution)/shard_map/pallas_call | solution.py:710
  46.7 2.7 %shard_map.51 = (f32[256,510]{1,0:T(8,128)}, f32[768,1536]{1,0:T(8,128)}) custom-call(f32[256,510]{1,0:T(8,128)S(1)} %get-tuple-element.8.spec_in, f32[768,1536]{1,0:T(8,128)S(1)} %get-tuple-element.9.low_in, bf16[4,192,512]{2,1,0:T(8,128)(2,1)S(1)} %get-tuple-element.10.wide_in, bf16[1536,512]{1,0:T(8,128)(2,1)S(1)} %get-tuple-element.11.y_in), custom_call_target="tpu_custom_call" | custom-call | tf_op jit(solution)/shard_map/pallas_call | solution.py:792

commit v7 on v6

--- a/solution.py
+++ b/solution.py
@@ -631,10 +631,12 @@
                     with scope("fwdwait"):
                         all_forward(last - 2, peer).wait_recv()
                 if m < pieces - 1:
-                    for f in range(m * lead // (pieces - 1), (m + 1) * lead // (pieces - 1)):
+                    for f in range(m, min(m + 1, lead)):
                         add_field(last - 2, f)
             synthesis(last)
             forward(last, spot, half).start()
+            for f in range(pieces - 1, lead):
+                add_field(last - 2, f)
 
         take(last - 1)
         @pl.when(half == 0)

time: 49.8 us -> 49.8 us (level)
  no operation moved by 1% of the time
where the time goes in v7:
time: 49.8 us; the launch traced here: 49.6 us
  Pallas kernels  48.8 us (98%)
  between operations  0.8 us (2%)
    pallas_call x1, Pallas kernels, spectral_filter(): pl.pallas_call(functools.partial(filter_kernel, lead, x_local, kx, ky, kp...  46.1 us
    pallas_call x1, Pallas kernels, last_sum(): pl.pallas_call(functools.partial(last_sum_kernel, near_first(lead)), out_...  2.75 us

profile of v7, /device:TPU:0, one launch (start us, length us, event | category | flops | bytes accessed | tf_op | source)
XLA Modules:
  0.0 49.6 jit_solution(18008413652318975595)
XLA Ops:
  0.6 46.1 %shard_map.50 = (f32[256,510]{1,0:T(8,128)S(1)}, f32[768,1536]{1,0:T(8,128)S(1)}, bf16[4,192,512]{2,1,0:T(8,128)(2,1)S(1)}, bf16[1536,512]{1,0:T(8,128)(2,1)S(1)}) custom-call(bf16[768,1536]{1,0:T(8,128)(2,1)} %bitcast.9, s32[1,1024]{1,0:T(1,128)} %bitcast.10, s32[1,1020]{1,0:T(1,128)} %bitcast.11), custom_call_target="tpu_custom_call" | custom-call | tf_op jit(solution)/shard_map/pallas_call | solution.py:712
  46.7 2.7 %shard_map.51 = (f32[256,510]{1,0:T(8,128)}, f32[768,1536]{1,0:T(8,128)}) custom-call(f32[256,510]{1,0:T(8,128)S(1)} %get-tuple-element.8.spec_in, f32[768,1536]{1,0:T(8,128)S(1)} %get-tuple-element.9.low_in, bf16[4,192,512]{2,1,0:T(8,128)(2,1)S(1)} %get-tuple-element.10.wide_in, bf16[1536,512]{1,0:T(8,128)(2,1)S(1)} %get-tuple-element.11.y_in), custom_call_target="tpu_custom_call" | custom-call | tf_op jit(solution)/shard_map/pallas_call | solution.py:794
